TPU v7x, 32 devices: a whole 2x2x4 slice. The times are simulated.
32 devices in a mesh: gx: 2 (over y), gy: 4 (over x, core), gz: 4 (over z).
Axes of the slice: x: 2, y: 2, z: 4, core: 2. Of those that a mesh axis runs over, the one named last changes fastest.
Arguments:
- species: float32 [5, 8, 32, 512], P(None, 'gx', 'gy', 'gz'), may hold values from 0.09 to 0.6
- velocity_in: float32 [3, 8, 32, 512], P(None, 'gx', 'gy', 'gz'), may hold values from -3 to 3
- pressure_in: float32 [8, 32, 512], P('gx', 'gy', 'gz'), may hold values from 0.125 to 1
- wall_types: int32 [3, 2, 8, 128], P(None, 'gx', 'gy', 'gz'), may hold values 0 or 1
Outputs:
- new_state: float32 [9, 8, 32, 512], P(None, 'gx', 'gy', 'gz')
- blending: float32 [2, 8, 128], P('gx', 'gy', 'gz')
All inputs are finite; a program needn't handle non-finite values. Where the computation divides by a largest or mean magnitude, that divisor is 1e-20 or more. No bound on the sum of `wall_types` on one device may be relied on, other than what follows from the above.
Results may differ from a plain program's by a relative error of at most 0.0003.
Values sent between devices are 32-bit elements; how exact they have to be, the bound alone decides.
A program may use at most 64 MiB of HBM per device.

v0:
```python
import functools
import itertools

import jax
import jax.numpy as jnp
from jax import lax
from jax.experimental import pallas as pl
from jax.experimental.pallas import tpu as pltpu
from jax.sharding import PartitionSpec as P

SPECIES = 5
P_SIZE = 4
ITERS = 2
GAMMA = 1.4
COURANT = 0.4
FLOOR = 0.1
SLOPE_FLOOR = 0.01
SPREAD = 0.002
RELAX = 0.1

COMPS = SPECIES + 4
AXES = ("gx", "gy", "gz")
ROW = 128
DIRECT = 64
MESH = pl.DeviceIdType.MESH


def reduce_groups(sizes):
    if sizes[0] * sizes[1] * sizes[2] <= DIRECT:
        return [(0, 1, 2)]
    return [(2,), (1,), (0,)]


def group_offsets(sizes, group):
    spans = [range(sizes[d]) if d in group else (0,) for d in range(3)]
    return [off for off in itertools.product(*spans)]


def conserved_of(inputs):
    species, velocity, pressure = inputs[:SPECIES], inputs[SPECIES : SPECIES + 3], inputs[-1]
    density = sum(species[1:], species[0])
    square = velocity[0] * velocity[0] + velocity[1] * velocity[1] + velocity[2] * velocity[2]
    energy = pressure * (1.0 / (GAMMA - 1.0)) + 0.5 * density * square
    return list(species) + [density * v for v in velocity] + [energy]


def primitives(cons):
    density = sum(cons[1:SPECIES], cons[0])
    safe = jnp.maximum(density, FLOOR)
    inverse = 1.0 / safe
    momentum = cons[SPECIES : SPECIES + 3]
    velocity = [m * inverse for m in momentum]
    kinetic = momentum[0] * velocity[0] + momentum[1] * velocity[1] + momentum[2] * velocity[2]
    pressure = (GAMMA - 1.0) * (cons[SPECIES + 3] - 0.5 * kinetic)
    return density, safe, inverse, velocity, pressure


def sound_of(inverse, pressure):
    return jnp.sqrt(GAMMA * jnp.maximum(pressure, FLOOR) * inverse)


def entropy(density, safe, pressure):
    return density * (jnp.log(jnp.maximum(pressure, FLOOR)) - GAMMA * jnp.log(safe))


def flux_term(cons, velocity, pressure, comp, d):
    term = cons[comp] * velocity[d]
    if comp == SPECIES + d:
        term = term + pressure
    if comp == SPECIES + 3:
        term = term + pressure * velocity[d]
    return term


def face_pair(mm, left, right, pp, jump, rate, wall, wall_value):
    both = left + right
    high = (7.0 * both - (mm + pp)) * (1.0 / 12.0)
    low = 0.5 * both - rate * jump
    keep = 0.0 if wall_value is None else wall_value
    diff = jnp.where(wall, 0.0, high - low)
    return jnp.where(wall, keep, low), diff


def kernel(
    sizes, sp_hbm, ve_hbm, pr_hbm, wa_hbm, out, bl, sp, ve, pr, wa, load_sem,
    xsp, xve, xpr, ys, yr, hy, zs, zr, es, er, pk, pn, pz, qz,
    dx, du, dw, lows, deltas, halo_send, halo_recv, *reduce_scratch
):
    X, Y, Z = pr.shape
    EX, EY, EZ = wa.shape[1:]
    loads = [
        pltpu.make_async_copy(source, target, load_sem.at[i])
        for i, (source, target) in enumerate(
            ((sp_hbm, sp), (ve_hbm, ve), (pr_hbm, pr), (wa_hbm, wa))
        )
    ]
    for copy in loads:
        copy.start()
    me = [lax.axis_index(name) for name in AXES]
    groups = reduce_groups(sizes)

    place = [[me[d]] + [lax.rem(me[d] + k, sizes[d]) for k in range(1, sizes[d])] for d in range(3)]

    def device(off):
        return tuple(place[d][off[d]] for d in range(3))

    def step(d, k):
        return tuple(k % sizes[d] if a == d else 0 for a in range(3))

    peers = {step(d, k) for d in range(3) for k in (1, -1)}
    for group in groups:
        peers |= set(group_offsets(sizes, group))
    peers.discard((0, 0, 0))
    barrier = pltpu.get_barrier_semaphore()
    for off in sorted(peers):
        pl.semaphore_signal(barrier, inc=1, device_id=device(off), device_id_type=MESH)
    for copy in loads:
        copy.wait()

    started = []

    def send(src, dst, slot, off):
        copy = pltpu.make_async_remote_copy(
            src_ref=src,
            dst_ref=dst,
            send_sem=halo_send.at[slot],
            recv_sem=halo_recv.at[slot],
            device_id=device(off),
            device_id_type=MESH,
        )
        copy.start()
        started.append(copy)
        return copy

    def spread_start(turn, stage, row):
        base = 3 * (turn * len(groups) + stage)
        buf, ssem, rsem = reduce_scratch[base : base + 3]
        buf[0] = row
        copies = []
        for i, off in enumerate(group_offsets(sizes, groups[stage])):
            if i == 0:
                continue
            copy = pltpu.make_async_remote_copy(
                src_ref=buf.at[0],
                dst_ref=buf.at[i],
                send_sem=ssem.at[i],
                recv_sem=rsem.at[i],
                device_id=device(off),
                device_id_type=MESH,
            )
            copy.start()
            copies.append(copy)
        started.extend(copies)
        return buf, copies

    def spread_end(turn, begun, combine):
        for stage in range(len(groups)):
            if stage > 0:
                begun = spread_start(turn, stage, row)
            buf, copies = begun
            for copy in copies:
                copy.wait_recv()
            row = combine(buf[...])
        return row

    row_index = lax.broadcasted_iota(jnp.int32, (1, Y, Z), 1)
    lane_index = lax.broadcasted_iota(jnp.int32, (1, Y, Z), 2)
    index = {1: row_index, 2: lane_index}
    extent = {1: Y, 2: Z}

    def roll(value, shift, axis):
        return pltpu.roll(value, shift % value.shape[axis], axis)

    def mesh_group(value, axis, op):
        for s in (1, 2):
            low = (index[axis] & s) == 0
            value = op(value, jnp.where(low, roll(value, -s, axis), roll(value, s, axis)))
        return value

    def element(value, op):
        parts = value.reshape(EX, P_SIZE, Y, Z)
        value = op(op(parts[:, 0], parts[:, 1]), op(parts[:, 2], parts[:, 3]))
        return mesh_group(mesh_group(value, 1, op), 2, op)

    def nodes(value):
        return jnp.broadcast_to(value[:, None], (EX, P_SIZE, Y, Z)).reshape(X, Y, Z)

    def total(value, op):
        value = functools.reduce(op, [value[x] for x in range(X)])
        value = {jnp.minimum: jnp.min, jnp.maximum: jnp.max, jnp.add: jnp.sum}[op](
            value, axis=0, keepdims=True
        )
        return {jnp.minimum: jnp.min, jnp.maximum: jnp.max, jnp.add: jnp.sum}[op](
            value, axis=1, keepdims=True
        )

    def block(comp):
        if comp < SPECIES:
            return sp[comp]
        if comp < SPECIES + 3:
            return ve[comp - SPECIES]
        return pr[...]

    own_inputs = [block(c) for c in range(COMPS)]

    cons = conserved_of(own_inputs)
    density, _, inverse, velocity, pressure = primitives(cons)
    sound = sound_of(inverse, pressure)
    speed = jnp.abs(velocity[0]) + jnp.abs(velocity[1]) + jnp.abs(velocity[2]) + 3.0 * sound
    speed_row = jnp.broadcast_to(total(speed, jnp.maximum), (1, ROW))

    for c in range(COMPS):
        for x in range(X):
            ys[0, c, 2 * x : 2 * x + 2, :] = own_inputs[c][x, Y - 2 : Y, :]
            ys[1, c, 2 * x : 2 * x + 2, :] = own_inputs[c][x, 0:2, :]
    packs = zs.shape[0]
    per_pack = Z // (4 * X)
    for v in range(packs):
        packed = jnp.zeros((1, Y, Z), jnp.float32)
        for c in range(v * per_pack, min((v + 1) * per_pack, COMPS)):
            for x in range(X):
                at = ((c - v * per_pack) * X + x) * 4
                moved = roll(own_inputs[c][x : x + 1], at + 2, 2)
                packed = jnp.where((lane_index >= at) & (lane_index < at + 4), moved, packed)
        zs[v] = packed[0]

    rho_min = element(density, jnp.minimum)
    p_min = element(pressure, jnp.minimum)
    widen = (
        lax.broadcasted_iota(jnp.int32, (EZ, Z), 1) // P_SIZE
        == lax.broadcasted_iota(jnp.int32, (EZ, Z), 0)
    ).astype(jnp.float32)
    heighten = (
        lax.broadcasted_iota(jnp.int32, (Y, EY), 0) // P_SIZE
        == lax.broadcasted_iota(jnp.int32, (Y, EY), 1)
    ).astype(jnp.float32)
    walls = []
    for d in range(3):
        layers = []
        for e in range(EX):
            flags = wa[d, e].astype(jnp.float32)
            flags = jnp.dot(flags, widen, preferred_element_type=jnp.float32)
            layers.append(jnp.dot(heighten, flags, preferred_element_type=jnp.float32)[None])
        walls.append(jnp.concatenate(layers, axis=0))
        es[d, 0] = rho_min
        es[d, 1] = p_min
        es[d, 2] = walls[d]

    pl.semaphore_wait(barrier, len(peers))

    speed_begun = spread_start(0, 0, speed_row)
    arrivals = {}
    for side, k in ((0, 1), (1, -1)):
        arrivals["z", side] = [send(zs, zr.at[side], 8 + side, step(2, k))]
        arrivals["y", side] = [send(ys.at[side], yr.at[side], 6 + side, step(1, k))]
        for d in (2, 1, 0):
            arrivals["e", d, side] = [send(es.at[d], er.at[side, d], 10 + 2 * d + side, step(d, k))]
    for side, k in ((0, 1), (1, -1)):
        at = X - 2 if side == 0 else 0
        off = step(0, k)
        arrivals["x", side] = [
            send(sp.at[:, at : at + 2], xsp.at[side], 3 * side, off),
            send(ve.at[:, at : at + 2], xve.at[side], 3 * side + 1, off),
            send(pr.at[at : at + 2], xpr.at[side], 3 * side + 2, off),
        ]

    def arrive(*key):
        for copy in arrivals[key]:
            copy.wait_recv()

    def cyclic_fluxes(d, halo_inputs, number):
        n = extent[d]
        ix = index[d]
        halo = conserved_of(halo_inputs)
        _, _, h_inv, h_vel, h_p = primitives(halo)
        h_rate = jnp.abs(h_vel[d]) + sound_of(h_inv, h_p)
        rate = jnp.abs(velocity[d]) + sound
        first, last = ix == 0, ix == n - 1
        two_first, two_last = ix < 2, ix >= n - 2

        def right_of(value, beyond):
            return roll(jnp.where(first, beyond, value), -1, d)

        arrive("e", d, 0)
        arrive("e", d, 1)
        flag = right_of(walls[d], er[1, d, 2])
        flag_low = roll(walls[d], -1, d)
        ends = (ix & (P_SIZE - 1)) == P_SIZE - 1
        wall = nodes(jnp.where(ends, flag, 0.0)) > 0.5
        wall_low = nodes(jnp.where(ends, flag_low, 0.0)) > 0.5
        half_rate = 0.5 * jnp.maximum(rate, right_of(rate, h_rate))
        half_low = 0.5 * jnp.maximum(h_rate, roll(rate, -1, d))
        wall_p = 0.5 * (pressure + right_of(pressure, h_p))
        wall_p_low = 0.5 * (h_p + roll(pressure, -1, d))
        for c in range(COMPS):
            f = flux_term(cons, velocity, pressure, c, d)
            h = flux_term(halo, h_vel, h_p, c, d)
            is_normal = c == SPECIES + d
            low, diff = face_pair(
                roll(jnp.where(last, h, f), 1, d),
                f,
                right_of(f, h),
                roll(jnp.where(two_first, h, f), -2, d),
                right_of(cons[c], halo[c]) - cons[c],
                half_rate,
                wall,
                wall_p if is_normal else None,
            )
            edge_low, edge_diff = face_pair(
                roll(h, 1, d),
                h,
                roll(f, -1, d),
                roll(f, -2, d),
                roll(cons[c], -1, d) - halo[c],
                half_low,
                wall_low,
                wall_p_low if is_normal else None,
            )
            before_low = roll(jnp.where(last, edge_low, low), 1, d)
            before_diff = roll(jnp.where(last, edge_diff, diff), 1, d)
            du[number, c] = diff
            dw[number, c] = before_diff
            if number == 0:
                lows[c] = low - before_low
                deltas[c] = diff - before_diff
            else:
                lows[c] += low - before_low
                deltas[c] += diff - before_diff

    arrive("z", 0)
    arrive("z", 1)
    merged = [
        jnp.where((lane_index & 3) < 2, zr[0, v][None], zr[1, v][None]) for v in range(packs)
    ]
    z_halo = []
    for c in range(COMPS):
        layers = []
        for x in range(X):
            at = ((c % per_pack) * X + x) * 4
            layers.append(roll(merged[c // per_pack], -(at + 2), 2))
        z_halo.append(jnp.concatenate(layers, axis=0))
    cyclic_fluxes(2, z_halo, 0)

    arrive("y", 0)
    arrive("y", 1)
    for c in range(COMPS):
        hy[c] = own_inputs[c]
        for x in range(X):
            hy[c, x, Y - 2 : Y, :] = yr[0, c, 2 * x : 2 * x + 2, :]
            hy[c, x, 0:2, :] = yr[1, c, 2 * x : 2 * x + 2, :]
    cyclic_fluxes(1, [hy[c] for c in range(COMPS)], 1)

    for side in (0, 1):
        arrive("x", side)
        arrive("e", 0, side)
    sides = []
    for side in (0, 1):
        inputs = [xsp[side, c] for c in range(SPECIES)]
        inputs += [xve[side, c] for c in range(3)]
        inputs.append(xpr[side])
        halo = conserved_of(inputs)
        _, _, h_inv, h_vel, h_p = primitives(halo)
        sides.append((halo, h_vel, h_p, jnp.abs(h_vel[0]) + sound_of(h_inv, h_p)))

    def joined(below, own, above):
        return jnp.concatenate([below, own, above], axis=0)

    rate = joined(sides[0][3], jnp.abs(velocity[0]) + sound, sides[1][3])
    p_ext = joined(sides[0][2], pressure, sides[1][2])
    half_rate = 0.5 * jnp.maximum(rate[1 : X + 2], rate[2 : X + 3])
    wall_p = 0.5 * (p_ext[1 : X + 2] + p_ext[2 : X + 3])
    planes = []
    for x in range(-1, X):
        if (x + 1) % P_SIZE:
            planes.append(jnp.zeros((1, Y, Z), jnp.float32))
        elif x == X - 1:
            planes.append(er[1, 0, 2, 0:1])
        else:
            e = (x + 1) // P_SIZE
            planes.append(walls[0][e : e + 1])
    wall = jnp.concatenate(planes, axis=0) > 0.5
    for c in range(COMPS):
        f = joined(
            flux_term(sides[0][0], sides[0][1], sides[0][2], c, 0),
            flux_term(cons, velocity, pressure, c, 0),
            flux_term(sides[1][0], sides[1][1], sides[1][2], c, 0),
        )
        u = joined(sides[0][0][c], cons[c], sides[1][0][c])
        low, diff = face_pair(
            f[0 : X + 1],
            f[1 : X + 2],
            f[2 : X + 3],
            f[3 : X + 4],
            u[2 : X + 3] - u[1 : X + 2],
            half_rate,
            wall,
            wall_p if c == SPECIES else None,
        )
        dx[c] = diff
        lows[c] += low[1:] - low[:-1]
        deltas[c] += diff[1:] - diff[:-1]

    def bound(own, which):
        best = own
        for d in (1, 2):
            n = extent[d]
            up = jnp.where(index[d] < P_SIZE, er[1, d, which], own)
            down = jnp.where(index[d] >= n - P_SIZE, er[0, d, which], own)
            best = jnp.minimum(best, jnp.minimum(roll(up, -P_SIZE, d), roll(down, P_SIZE, d)))
        chain = joined(er[0, 0, which, EX - 1 : EX], own, er[1, 0, which, 0:1])
        return jnp.minimum(best, jnp.minimum(chain[:EX], chain[2:]))

    rho_bound = bound(rho_min, 0)
    p_bound = bound(p_min, 1)

    speed_max = spread_end(0, speed_begun, lambda rows: jnp.max(rows, axis=0))
    ratio = (COURANT / speed_max)[0:1, 0:1].reshape(1, 1, 1)

    for c in range(COMPS):
        lows[c] = cons[c] - ratio * lows[c]
        deltas[c] = -(ratio * deltas[c])
    low_density, low_safe, _, _, low_pressure = primitives([lows[c] for c in range(COMPS)])
    low_sigma = entropy(low_density, low_safe, low_pressure)
    d_rho = sum([deltas[c] for c in range(1, SPECIES)], deltas[0])
    rho_scale = 1.0 / jnp.maximum(-d_rho, SLOPE_FLOOR)
    count = X * Y * Z * sizes[0] * sizes[1] * sizes[2]
    stat_lane = lax.broadcasted_iota(jnp.int32, (1, ROW), 1)

    def combine_stats(rows):
        return jnp.where(stat_lane < 2, jnp.min(rows, axis=0), jnp.sum(rows, axis=0))

    def next_blend(got, packed):
        t_density, rho_scale, t_p, p_scale, rho_bound, p_bound, mean_square, base = packed
        lowest_rho = got[0:1, 0:1].reshape(1, 1, 1)
        lowest_p = got[0:1, 1:2].reshape(1, 1, 1)
        spread = got[0:1, 2:3].reshape(1, 1, 1) * (1.0 / count) + SPREAD
        rho_target = rho_bound - RELAX * jnp.maximum(rho_bound - lowest_rho, 0.0)
        p_target = p_bound - RELAX * jnp.maximum(p_bound - lowest_p, 0.0)
        step_rho = jnp.minimum(t_density - nodes(rho_target), 0.0) * rho_scale
        step_p = jnp.minimum(t_p - nodes(p_target), 0.0) * p_scale
        lowered = element(jnp.minimum(step_rho, step_p), jnp.minimum)
        cap = spread / (spread + mean_square)
        return jnp.maximum(jnp.minimum(cap, base + lowered), 0.0)

    per_edge = Z // (2 * P_SIZE)
    blend = None
    for newton in range(ITERS):
        blend_nodes = None if blend is None else nodes(blend)
        trial = [
            lows[c] + (deltas[c] if blend is None else blend_nodes * deltas[c])
            for c in range(COMPS)
        ]
        t_density, t_safe, _, t_vel, t_p = primitives(trial)
        residual = entropy(t_density, t_safe, t_p) - low_sigma
        square = residual * residual
        stats = jnp.where(
            stat_lane == 0,
            total(t_density, jnp.minimum),
            jnp.where(stat_lane == 1, total(t_p, jnp.minimum), total(square, jnp.add)),
        )
        begun = spread_start(newton + 1, 0, stats)
        cross = sum([t_vel[k] * deltas[SPECIES + k] for k in range(1, 3)], t_vel[0] * deltas[SPECIES])
        speed2 = t_vel[0] * t_vel[0] + t_vel[1] * t_vel[1] + t_vel[2] * t_vel[2]
        slope = (GAMMA - 1.0) * (deltas[SPECIES + 3] - cross + 0.5 * speed2 * d_rho)
        p_scale = 1.0 / jnp.maximum(-slope, SLOPE_FLOOR)
        mean_square = element(square, jnp.add) * (1.0 / (P_SIZE**3))
        base = jnp.ones((EX, Y, Z), jnp.float32) if blend is None else blend
        if newton == ITERS - 1:
            fields = (t_density, rho_scale, t_p, p_scale)
            for i, value in enumerate(fields):
                pk[i * X : (i + 1) * X] = value
            for i, value in enumerate((rho_bound, p_bound, mean_square, base)):
                pk[4 * X + i * EX : 4 * X + (i + 1) * EX] = value
            items = [value[x : x + 1] for value in fields for x in range(X)]
            for value in (rho_bound, p_bound, mean_square, base):
                items += [value[e : e + 1] for e in range(EX)]
            for v in range(pz.shape[0]):
                packed = jnp.zeros((1, Y, Z), jnp.float32)
                for j, item in enumerate(items[v * per_edge : (v + 1) * per_edge]):
                    at = 2 * P_SIZE * j
                    moved = roll(item, at + P_SIZE, 2)
                    inside = (lane_index >= at) & (lane_index < at + 2 * P_SIZE)
                    packed = jnp.where(inside, moved, packed)
                pz[v] = packed[0]
            for side, k in ((0, 1), (1, -1)):
                arrivals["b", 2, side] = [send(pz, qz.at[side], 20 + side, step(2, k))]
            for d in (0, 1):
                for side, k in ((0, 1), (1, -1)):
                    if side == 0 or sizes[d] > 2:
                        copy = send(pk, pn.at[side, d], 16 + 2 * d + side, step(d, k))
                        arrivals["b", d, side] = [copy]
                    else:
                        arrivals["b", d, side] = []
        got = spread_end(newton + 1, begun, combine_stats)
        blend = next_blend(
            got, (t_density, rho_scale, t_p, p_scale, rho_bound, p_bound, mean_square, base)
        )

    beside = {}
    arrive("b", 2, 0)
    arrive("b", 2, 1)
    near = (lane_index & (2 * P_SIZE - 1)) < P_SIZE
    edges = [jnp.where(near, qz[0, v][None], qz[1, v][None]) for v in range(qz.shape[1])]
    items = [
        roll(edges[j // per_edge], -(2 * P_SIZE * (j % per_edge) + P_SIZE), 2)
        for j in range(4 * X + 4 * EX)
    ]
    packed = [jnp.concatenate(items[i * X : (i + 1) * X], axis=0) for i in range(4)]
    packed += [
        jnp.concatenate(items[4 * X + i * EX : 4 * X + (i + 1) * EX], axis=0) for i in range(4)
    ]
    beside[2, 0] = beside[2, 1] = next_blend(got, packed)
    for d in (0, 1):
        for side in (0, 1):
            arrive("b", d, side)
            if side == 1 and sizes[d] == 2:
                beside[d, side] = beside[d, 0]
                continue
            packed = [pn[side, d, i * X : (i + 1) * X] for i in range(4)]
            packed += [pn[side, d, 4 * X + i * EX : 4 * X + (i + 1) * EX] for i in range(4)]
            beside[d, side] = next_blend(got, packed)

    pick_lanes = (
        lax.broadcasted_iota(jnp.int32, (Z, EZ), 1) * P_SIZE
        == lax.broadcasted_iota(jnp.int32, (Z, EZ), 0)
    ).astype(jnp.float32)
    for e in range(EX):
        few = jnp.dot(
            blend[e], pick_lanes, preferred_element_type=jnp.float32, precision=lax.Precision.HIGHEST
        )
        bl[e] = jnp.concatenate([few[j * P_SIZE : j * P_SIZE + 1] for j in range(EY)], axis=0)

    theta = []
    for d in (2, 1):
        above = roll(jnp.where(index[d] == 0, beside[d, 1], blend), -1, d)
        below = roll(jnp.where(index[d] == extent[d] - 1, beside[d, 0], blend), 1, d)
        theta.append((nodes(jnp.minimum(blend, above)), nodes(jnp.minimum(blend, below))))
    x_blend = joined(beside[0, 0][EX - 1 : EX], nodes(blend), beside[0, 1][0:1])
    x_theta = jnp.minimum(x_blend[:-1], x_blend[1:])
    for c in range(COMPS):
        faces = x_theta * dx[c]
        change = faces[1:] - faces[:-1]
        for number in range(2):
            upper, lower = theta[number]
            change += upper * du[number, c] - lower * dw[number, c]
        out[c] = lows[c] - ratio * change

    for copy in started:
        copy.wait_send()


def solution(mesh):
    sizes = tuple(mesh.shape[name] for name in AXES)

    def local(species, velocity_in, pressure_in, wall_types):
        X, Y, Z = pressure_in.shape
        EX, EY, EZ = wall_types.shape[1:]
        packs = -(-COMPS // (Z // (4 * X)))
        edge_packs = -(-(4 * X + 4 * EX) // (Z // (2 * P_SIZE)))
        vmem = lambda *shape: pltpu.VMEM(shape, jnp.float32)
        reduce_scratch = []
        for _ in range(ITERS + 1):
            for group in reduce_groups(sizes):
                n = len(group_offsets(sizes, group))
                reduce_scratch += [
                    vmem(n, 1, ROW),
                    pltpu.SemaphoreType.DMA((n,)),
                    pltpu.SemaphoreType.DMA((n,)),
                ]
        return tuple(
            pl.pallas_call(
                functools.partial(kernel, sizes),
                out_shape=[
                    pltpu.VMEM((COMPS, X, Y, Z), jnp.float32),
                    pltpu.VMEM((EX, EY, EZ), jnp.float32),
                ],
                in_specs=[pl.BlockSpec(memory_space=pltpu.HBM)] * 4,
                out_specs=[pl.BlockSpec(memory_space=pltpu.VMEM)] * 2,
                scratch_shapes=[
                    vmem(SPECIES, X, Y, Z),
                    vmem(3, X, Y, Z),
                    vmem(X, Y, Z),
                    pltpu.VMEM((3, EX, EY, EZ), jnp.int32),
                    pltpu.SemaphoreType.DMA((4,)),
                    vmem(2, SPECIES, 2, Y, Z),
                    vmem(2, 3, 2, Y, Z),
                    vmem(2, 2, Y, Z),
                    vmem(2, COMPS, 2 * X, Z),
                    vmem(2, COMPS, 2 * X, Z),
                    vmem(COMPS, X, Y, Z),
                    vmem(packs, Y, Z),
                    vmem(2, packs, Y, Z),
                    vmem(3, 3, EX, Y, Z),
                    vmem(2, 3, 3, EX, Y, Z),
                    vmem(4 * X + 4 * EX, Y, Z),
                    vmem(2, 2, 4 * X + 4 * EX, Y, Z),
                    vmem(edge_packs, Y, Z),
                    vmem(2, edge_packs, Y, Z),
                    vmem(COMPS, X + 1, Y, Z),
                    vmem(2, COMPS, X, Y, Z),
                    vmem(2, COMPS, X, Y, Z),
                    vmem(COMPS, X, Y, Z),
                    vmem(COMPS, X, Y, Z),
                    pltpu.SemaphoreType.DMA((22,)),
                    pltpu.SemaphoreType.DMA((22,)),
                ]
                + reduce_scratch,
                compiler_params=pltpu.CompilerParams(collective_id=0, has_side_effects=True),
            )(species, velocity_in, pressure_in, wall_types)
        )

    in_specs = (
        P(None, "gx", "gy", "gz"),
        P(None, "gx", "gy", "gz"),
        P("gx", "gy", "gz"),
        P(None, "gx", "gy", "gz"),
    )
    out_specs = (P(None, "gx", "gy", "gz"), P("gx", "gy", "gz"))
    return jax.shard_map(local, mesh=mesh, in_specs=in_specs, out_specs=out_specs, check_vma=False)
```

profile of v0, /device:TPU:0, one launch (start us, length us, event | category | flops | bytes accessed | tf_op | source)
XLA Modules:
  0.0 27.8 jit_solution(10701033363484933773)
XLA Ops:
  0.6 25.9 %shard_map.59 = (f32[9,4,8,128]{3,2,1,0:T(8,128)S(1)}, f32[1,2,32]{2,1,0:T(2,128)S(1)}) custom-call(f32[5,4,8,128]{3,2,1,0:T(8,128)} %sp_hbm.1, f32[3,4,8,128]{3,2,1,0:T(8,128)} %ve_hbm.1, f32[4,8,128]{2,1,0:T(8,128)} %pr_hbm.1, s32[3,1,2,32]{3,2,1,0:T(2,128)} %wa_hbm.1), custom_call_target="tpu_custom_call" | custom-call | tf_op jit(solution)/shard_map/pallas_call | solution.py:571
  26.5 0.7 %copy.8 = f32[9,4,8,128]{3,2,1,0:T(8,128)} copy(f32[9,4,8,128]{3,2,1,0:T(8,128)S(1)} %get-tuple-element.2) | data formatting | bytes 294912
  27.2 0.6 %copy.9 = f32[1,2,32]{2,1,0:T(2,128)} copy(f32[1,2,32]{2,1,0:T(2,128)S(1)} %get-tuple-element.3) | data formatting | bytes 512
where the time goes:
time: 27.9 us; the launch traced here: 27.8 us
  Pallas kernels  25.9 us (93%)
  local copies, waits for them, and re-layouts  1.23 us (4%)
  between operations  0.64 us (2%)
    pallas_call x1, Pallas kernels, local(): pl.pallas_call(functools.partial(kernel, sizes), out_shape=[pltpu.VMEM((C...  25.9 us
    unnamed x2, local copies, waits for them, and re-layouts  1.23 us

commit v1 on v0

--- a/solution.py
+++ b/solution.py
@@ -33,7 +33,12 @@
 
 def group_offsets(sizes, group):
     spans = [range(sizes[d]) if d in group else (0,) for d in range(3)]
-    return [off for off in itertools.product(*spans)]
+    far = lambda off: sum(min(off[d], sizes[d] - off[d]) for d in range(3))
+    return sorted(itertools.product(*spans), key=far)
+
+
+def halo_links(sizes):
+    return [(d, k) for d in range(3) for k in ((1,) if sizes[d] == 2 else (1, -1))]
 
 
 def conserved_of(inputs):
@@ -84,7 +89,7 @@
 def kernel(
     sizes, sp_hbm, ve_hbm, pr_hbm, wa_hbm, out, bl, sp, ve, pr, wa, load_sem,
     xsp, xve, xpr, ys, yr, hy, zs, zr, es, er, pk, pn, pz, qz,
-    dx, du, dw, lows, deltas, halo_send, halo_recv, *reduce_scratch
+    dx, du, dw, lows, deltas, halo_send, halo_recv, near_sem, all_sem, *reduce_scratch
 ):
     X, Y, Z = pr.shape
     EX, EY, EZ = wa.shape[1:]
@@ -107,13 +112,75 @@
     def step(d, k):
         return tuple(k % sizes[d] if a == d else 0 for a in range(3))
 
-    peers = {step(d, k) for d in range(3) for k in (1, -1)}
-    for group in groups:
-        peers |= set(group_offsets(sizes, group))
-    peers.discard((0, 0, 0))
+    def traced(flag):
+        return jnp.where(flag, 1, 0).astype(jnp.int32)
+
+    links = halo_links(sizes)
+    near = {link: near_sem.at[i] for i, link in enumerate(links)}
+
+    def later(d, k):
+        return me[d] != sizes[d] - 1 if k == 1 else me[d] == 0
+
+    def neighbour(d, k):
+        return device(step(d, k))
+
+    corner = tuple(n - 1 for n in sizes)
+    is_corner = (me[0] == corner[0]) & (me[1] == corner[1]) & (me[2] == corner[2])
+    devices = sizes[0] * sizes[1] * sizes[2]
     barrier = pltpu.get_barrier_semaphore()
-    for off in sorted(peers):
-        pl.semaphore_signal(barrier, inc=1, device_id=device(off), device_id_type=MESH)
+
+    @pl.when(jnp.logical_not(is_corner))
+    def _():
+        pl.semaphore_signal(barrier, inc=1, device_id=corner, device_id_type=MESH)
+
+    expected = jnp.where(is_corner, devices - 1, 0).astype(jnp.int32)
+    for d, k in links:
+
+        @pl.when(later(d, k))
+        def _(d=d, k=k):
+            pl.semaphore_signal(barrier, inc=1, device_id=neighbour(d, k), device_id_type=MESH)
+
+        expected = expected + 1 - traced(later(d, k))
+
+    @pl.when(expected > 0)
+    def _():
+        pl.semaphore_wait(barrier, expected)
+
+    for d, k in links:
+        back = (d, k if sizes[d] == 2 else -k)
+
+        @pl.when(jnp.logical_not(later(d, k)))
+        def _(d=d, k=k, back=back):
+            pl.semaphore_signal(
+                near[back], inc=1, device_id=neighbour(d, k), device_id_type=MESH
+            )
+
+    @pl.when(is_corner)
+    def _():
+        def tell(i, carry):
+            z = lax.rem(i, sizes[2])
+            y = lax.rem(lax.div(i, sizes[2]), sizes[1])
+            x = lax.div(i, sizes[2] * sizes[1])
+            pl.semaphore_signal(all_sem, inc=1, device_id=(x, y, z), device_id_type=MESH)
+            return carry
+
+        if devices <= DIRECT:
+            for at in itertools.product(*[range(n) for n in sizes]):
+                if at != corner:
+                    pl.semaphore_signal(all_sem, inc=1, device_id=at, device_id_type=MESH)
+        else:
+            lax.fori_loop(0, devices - 1, tell, 0)
+
+    def await_near(d, k):
+        @pl.when(later(d, k))
+        def _():
+            pl.semaphore_wait(near[d, k], 1)
+
+    def await_all():
+        @pl.when(jnp.logical_not(is_corner))
+        def _():
+            pl.semaphore_wait(all_sem, 1)
+
     for copy in loads:
         copy.wait()
 
@@ -132,36 +199,68 @@
         started.append(copy)
         return copy
 
+    def spread_copy(turn, stage, i):
+        base = 4 * (turn * len(groups) + stage)
+        mine, buf, ssem, rsem = reduce_scratch[base : base + 4]
+        group = groups[stage]
+        off = group_offsets(sizes, group)[i]
+        there = tuple(
+            lax.rem(sizes[d] - 1 - me[d] + off[d], sizes[d]) if d in group else me[d]
+            for d in range(3)
+        )
+        can_be_me = all((off[d] + 1 - sizes[d]) % 2 == 0 or sizes[d] % 2 for d in group)
+        copy = pltpu.make_async_remote_copy(
+            src_ref=mine,
+            dst_ref=buf.at[pl.ds(i, 1)],
+            send_sem=ssem,
+            recv_sem=rsem,
+            device_id=there,
+            device_id_type=MESH,
+        )
+        return copy, can_be_me, functools.reduce(lambda a, b: a & b, [t == m for t, m in zip(there, me)])
+
     def spread_start(turn, stage, row):
-        base = 3 * (turn * len(groups) + stage)
-        buf, ssem, rsem = reduce_scratch[base : base + 3]
-        buf[0] = row
-        copies = []
-        for i, off in enumerate(group_offsets(sizes, groups[stage])):
-            if i == 0:
+        base = 4 * (turn * len(groups) + stage)
+        mine, buf = reduce_scratch[base : base + 2]
+        mine[...] = row
+        for i in range(buf.shape[0]):
+            copy, can_be_me, is_me = spread_copy(turn, stage, i)
+            if not can_be_me:
+                copy.start()
                 continue
-            copy = pltpu.make_async_remote_copy(
-                src_ref=buf.at[0],
-                dst_ref=buf.at[i],
-                send_sem=ssem.at[i],
-                recv_sem=rsem.at[i],
-                device_id=device(off),
-                device_id_type=MESH,
-            )
-            copy.start()
-            copies.append(copy)
-        started.extend(copies)
-        return buf, copies
-
-    def spread_end(turn, begun, combine):
+
+            @pl.when(jnp.logical_not(is_me))
+            def _(copy=copy):
+                copy.start()
+
+            @pl.when(is_me)
+            def _(i=i):
+                buf[i : i + 1] = row
+
+    def spread_whole(turn, stage):
+        base = 4 * (turn * len(groups) + stage)
+        _, buf, ssem, rsem = reduce_scratch[base : base + 4]
+        rows = buf.at[pl.ds(0, buf.shape[0] - 1)]
+        return pltpu.make_async_remote_copy(
+            src_ref=rows,
+            dst_ref=rows,
+            send_sem=ssem,
+            recv_sem=rsem,
+            device_id=device((1, 1, 1)),
+            device_id_type=MESH,
+        )
+
+    def spread_end(turn, combine):
         for stage in range(len(groups)):
             if stage > 0:
-                begun = spread_start(turn, stage, row)
-            buf, copies = begun
-            for copy in copies:
-                copy.wait_recv()
-            row = combine(buf[...])
+                spread_start(turn, stage, row)
+            spread_whole(turn, stage).wait_recv()
+            row = combine(reduce_scratch[4 * (turn * len(groups) + stage) + 1][...])
         return row
+
+    def spread_sent(turn):
+        for stage in range(len(groups)):
+            spread_whole(turn, stage).wait_send()
 
     row_index = lax.broadcasted_iota(jnp.int32, (1, Y, Z), 1)
     lane_index = lax.broadcasted_iota(jnp.int32, (1, Y, Z), 2)
@@ -246,23 +345,52 @@
         es[d, 1] = p_min
         es[d, 2] = walls[d]
 
-    pl.semaphore_wait(barrier, len(peers))
-
-    speed_begun = spread_start(0, 0, speed_row)
     arrivals = {}
-    for side, k in ((0, 1), (1, -1)):
-        arrivals["z", side] = [send(zs, zr.at[side], 8 + side, step(2, k))]
-        arrivals["y", side] = [send(ys.at[side], yr.at[side], 6 + side, step(1, k))]
-        for d in (2, 1, 0):
-            arrivals["e", d, side] = [send(es.at[d], er.at[side, d], 10 + 2 * d + side, step(d, k))]
+
+    def halo(key, src, dst, slot, off):
+        copy = pltpu.make_async_remote_copy(
+            src_ref=src,
+            dst_ref=dst,
+            send_sem=halo_send.at[slot],
+            recv_sem=halo_recv.at[slot],
+            device_id=device(off),
+            device_id_type=MESH,
+        )
+        arrivals.setdefault(key, []).append(copy)
+        started.append(copy)
+
     for side, k in ((0, 1), (1, -1)):
         at = X - 2 if side == 0 else 0
-        off = step(0, k)
-        arrivals["x", side] = [
-            send(sp.at[:, at : at + 2], xsp.at[side], 3 * side, off),
-            send(ve.at[:, at : at + 2], xve.at[side], 3 * side + 1, off),
-            send(pr.at[at : at + 2], xpr.at[side], 3 * side + 2, off),
-        ]
+        halo(("x", side), sp.at[:, at : at + 2], xsp.at[side], 3 * side, step(0, k))
+        halo(("x", side), ve.at[:, at : at + 2], xve.at[side], 3 * side + 1, step(0, k))
+        halo(("x", side), pr.at[at : at + 2], xpr.at[side], 3 * side + 2, step(0, k))
+        halo(("y", side), ys.at[side], yr.at[side], 6 + side, step(1, k))
+        halo(("z", side), zs, zr.at[side], 8 + side, step(2, k))
+        for d in range(3):
+            halo(("e", d, side), es.at[d], er.at[side, d], 10 + 2 * d + side, step(d, k))
+
+    def send_halo(d):
+        for side, k in ((0, 1), (1, -1)):
+            if (d, k) in links:
+                await_near(d, k)
+            for key in ((AXES[d][1], side), ("e", d, side)):
+                for copy in arrivals[key]:
+                    copy.start()
+
+    late = me[2] == sizes[2] - 1
+
+    @pl.when(jnp.logical_not(late))
+    def _():
+        send_halo(0)
+
+    send_halo(1)
+    send_halo(2)
+    await_all()
+    spread_start(0, 0, speed_row)
+
+    @pl.when(late)
+    def _():
+        send_halo(0)
 
     def arrive(*key):
         for copy in arrivals[key]:
@@ -413,7 +541,7 @@
     rho_bound = bound(rho_min, 0)
     p_bound = bound(p_min, 1)
 
-    speed_max = spread_end(0, speed_begun, lambda rows: jnp.max(rows, axis=0))
+    speed_max = spread_end(0, lambda rows: jnp.max(rows, axis=0, keepdims=True))
     ratio = (COURANT / speed_max)[0:1, 0:1].reshape(1, 1, 1)
 
     for c in range(COMPS):
@@ -427,7 +555,11 @@
     stat_lane = lax.broadcasted_iota(jnp.int32, (1, ROW), 1)
 
     def combine_stats(rows):
-        return jnp.where(stat_lane < 2, jnp.min(rows, axis=0), jnp.sum(rows, axis=0))
+        return jnp.where(
+            stat_lane < 2,
+            jnp.min(rows, axis=0, keepdims=True),
+            jnp.sum(rows, axis=0, keepdims=True),
+        )
 
     def next_blend(got, packed):
         t_density, rho_scale, t_p, p_scale, rho_bound, p_bound, mean_square, base = packed
@@ -458,7 +590,7 @@
             total(t_density, jnp.minimum),
             jnp.where(stat_lane == 1, total(t_p, jnp.minimum), total(square, jnp.add)),
         )
-        begun = spread_start(newton + 1, 0, stats)
+        spread_start(newton + 1, 0, stats)
         cross = sum([t_vel[k] * deltas[SPECIES + k] for k in range(1, 3)], t_vel[0] * deltas[SPECIES])
         speed2 = t_vel[0] * t_vel[0] + t_vel[1] * t_vel[1] + t_vel[2] * t_vel[2]
         slope = (GAMMA - 1.0) * (deltas[SPECIES + 3] - cross + 0.5 * speed2 * d_rho)
@@ -491,7 +623,7 @@
                         arrivals["b", d, side] = [copy]
                     else:
                         arrivals["b", d, side] = []
-        got = spread_end(newton + 1, begun, combine_stats)
+        got = spread_end(newton + 1, combine_stats)
         blend = next_blend(
             got, (t_density, rho_scale, t_p, p_scale, rho_bound, p_bound, mean_square, base)
         )
@@ -547,6 +679,8 @@
 
     for copy in started:
         copy.wait_send()
+    for turn in range(ITERS + 1):
+        spread_sent(turn)
 
 
 def solution(mesh):
@@ -563,9 +697,10 @@
             for group in reduce_groups(sizes):
                 n = len(group_offsets(sizes, group))
                 reduce_scratch += [
-                    vmem(n, 1, ROW),
-                    pltpu.SemaphoreType.DMA((n,)),
-                    pltpu.SemaphoreType.DMA((n,)),
+                    vmem(1, ROW),
+                    vmem(n, ROW),
+                    pltpu.SemaphoreType.DMA(()),
+                    pltpu.SemaphoreType.DMA(()),
                 ]
         return tuple(
             pl.pallas_call(
@@ -603,6 +738,8 @@
                     vmem(COMPS, X, Y, Z),
                     pltpu.SemaphoreType.DMA((22,)),
                     pltpu.SemaphoreType.DMA((22,)),
+                    pltpu.SemaphoreType.REGULAR((len(halo_links(sizes)),)),
+                    pltpu.SemaphoreType.REGULAR,
                 ]
                 + reduce_scratch,
                 compiler_params=pltpu.CompilerParams(collective_id=0, has_side_effects=True),

time: 27.9 us -> 23.6 us (0.85)
  Pallas kernels: 25.9 us -> 21.6 us
    pallas_call x1, Pallas kernels: 25.9 us -> 21.6 us  [local(): pl.pallas_call(functools.partial(kernel, sizes), out_shape=[pltpu.VMEM((C...]
where the time goes in v1:
time: 23.6 us; the launch traced here: 23.5 us
  Pallas kernels  21.6 us (92%)
  local copies, waits for them, and re-layouts  1.23 us (5%)
  between operations  0.64 us (3%)
    pallas_call x1, Pallas kernels, local(): pl.pallas_call(functools.partial(kernel, sizes), out_shape=[pltpu.VMEM((C...  21.6 us
    unnamed x2, local copies, waits for them, and re-layouts  1.23 us

profile of v1, /device:TPU:0, one launch (start us, length us, event | category | flops | bytes accessed | tf_op | source)
XLA Modules:
  0.0 23.5 jit_solution(4758718256512411172)
XLA Ops:
  0.6 21.6 %shard_map.59 = (f32[9,4,8,128]{3,2,1,0:T(8,128)S(1)}, f32[1,2,32]{2,1,0:T(2,128)S(1)}) custom-call(f32[5,4,8,128]{3,2,1,0:T(8,128)} %sp_hbm.1, f32[3,4,8,128]{3,2,1,0:T(8,128)} %ve_hbm.1, f32[4,8,128]{2,1,0:T(8,128)} %pr_hbm.1, s32[3,1,2,32]{3,2,1,0:T(2,128)} %wa_hbm.1), custom_call_target="tpu_custom_call" | custom-call | tf_op jit(solution)/shard_map/pallas_call | solution.py:706
  22.3 0.7 %copy.8 = f32[9,4,8,128]{3,2,1,0:T(8,128)} copy(f32[9,4,8,128]{3,2,1,0:T(8,128)S(1)} %get-tuple-element.2) | data formatting | bytes 294912
  22.9 0.6 %copy.9 = f32[1,2,32]{2,1,0:T(2,128)} copy(f32[1,2,32]{2,1,0:T(2,128)S(1)} %get-tuple-element.3) | data formatting | bytes 512

commit v2 on v1

--- a/solution.py
+++ b/solution.py
@@ -307,6 +307,14 @@
     sound = sound_of(inverse, pressure)
     speed = jnp.abs(velocity[0]) + jnp.abs(velocity[1]) + jnp.abs(velocity[2]) + 3.0 * sound
     speed_row = jnp.broadcast_to(total(speed, jnp.maximum), (1, ROW))
+    late = me[2] == corner[2]
+    last_chip = (me[0] == corner[0]) & (me[1] >= corner[1] - 1) & late
+
+    @pl.when(last_chip)
+    def _():
+        await_all()
+        spread_start(0, 0, speed_row)
+
 
     for c in range(COMPS):
         for x in range(X):
@@ -377,16 +385,21 @@
                 for copy in arrivals[key]:
                     copy.start()
 
-    late = me[2] == sizes[2] - 1
-
     @pl.when(jnp.logical_not(late))
     def _():
         send_halo(0)
-
-    send_halo(1)
+        send_halo(1)
+
     send_halo(2)
-    await_all()
-    spread_start(0, 0, speed_row)
+
+    @pl.when(late)
+    def _():
+        send_halo(1)
+
+    @pl.when(jnp.logical_not(last_chip))
+    def _():
+        await_all()
+        spread_start(0, 0, speed_row)
 
     @pl.when(late)
     def _():
@@ -396,18 +409,18 @@
         for copy in arrivals[key]:
             copy.wait_recv()
 
-    def cyclic_fluxes(d, halo_inputs, number):
+    def cyclic_fluxes(d, halo_inputs, number, first):
         n = extent[d]
         ix = index[d]
         halo = conserved_of(halo_inputs)
         _, _, h_inv, h_vel, h_p = primitives(halo)
         h_rate = jnp.abs(h_vel[d]) + sound_of(h_inv, h_p)
         rate = jnp.abs(velocity[d]) + sound
-        first, last = ix == 0, ix == n - 1
+        at_first, last = ix == 0, ix == n - 1
         two_first, two_last = ix < 2, ix >= n - 2
 
         def right_of(value, beyond):
-            return roll(jnp.where(first, beyond, value), -1, d)
+            return roll(jnp.where(at_first, beyond, value), -1, d)
 
         arrive("e", d, 0)
         arrive("e", d, 1)
@@ -448,12 +461,21 @@
             before_diff = roll(jnp.where(last, edge_diff, diff), 1, d)
             du[number, c] = diff
             dw[number, c] = before_diff
-            if number == 0:
+            if first:
                 lows[c] = low - before_low
                 deltas[c] = diff - before_diff
             else:
                 lows[c] += low - before_low
                 deltas[c] += diff - before_diff
+
+    arrive("y", 0)
+    arrive("y", 1)
+    for c in range(COMPS):
+        hy[c] = own_inputs[c]
+        for x in range(X):
+            hy[c, x, Y - 2 : Y, :] = yr[0, c, 2 * x : 2 * x + 2, :]
+            hy[c, x, 0:2, :] = yr[1, c, 2 * x : 2 * x + 2, :]
+    cyclic_fluxes(1, [hy[c] for c in range(COMPS)], 1, True)
 
     arrive("z", 0)
     arrive("z", 1)
@@ -467,16 +489,7 @@
             at = ((c % per_pack) * X + x) * 4
             layers.append(roll(merged[c // per_pack], -(at + 2), 2))
         z_halo.append(jnp.concatenate(layers, axis=0))
-    cyclic_fluxes(2, z_halo, 0)
-
-    arrive("y", 0)
-    arrive("y", 1)
-    for c in range(COMPS):
-        hy[c] = own_inputs[c]
-        for x in range(X):
-            hy[c, x, Y - 2 : Y, :] = yr[0, c, 2 * x : 2 * x + 2, :]
-            hy[c, x, 0:2, :] = yr[1, c, 2 * x : 2 * x + 2, :]
-    cyclic_fluxes(1, [hy[c] for c in range(COMPS)], 1)
+    cyclic_fluxes(2, z_halo, 0, False)
 
     for side in (0, 1):
         arrive("x", side)
@@ -683,6 +696,17 @@
         spread_sent(turn)
 
 
+def store(state, weights, state_hbm, weights_hbm, sem):
+    copies = [
+        pltpu.make_async_copy(state, state_hbm, sem.at[0]),
+        pltpu.make_async_copy(weights, weights_hbm, sem.at[1]),
+    ]
+    for copy in copies:
+        copy.start()
+    for copy in copies:
+        copy.wait()
+
+
 def solution(mesh):
     sizes = tuple(mesh.shape[name] for name in AXES)
 
@@ -702,7 +726,7 @@
                     pltpu.SemaphoreType.DMA(()),
                     pltpu.SemaphoreType.DMA(()),
                 ]
-        return tuple(
+        state, weights = (
             pl.pallas_call(
                 functools.partial(kernel, sizes),
                 out_shape=[
@@ -745,6 +769,18 @@
                 compiler_params=pltpu.CompilerParams(collective_id=0, has_side_effects=True),
             )(species, velocity_in, pressure_in, wall_types)
         )
+        return tuple(
+            pl.pallas_call(
+                store,
+                out_shape=[
+                    jax.ShapeDtypeStruct((COMPS, X, Y, Z), jnp.float32),
+                    jax.ShapeDtypeStruct((EX, EY, EZ), jnp.float32),
+                ],
+                in_specs=[pl.BlockSpec(memory_space=pltpu.VMEM)] * 2,
+                out_specs=[pl.BlockSpec(memory_space=pltpu.HBM)] * 2,
+                scratch_shapes=[pltpu.SemaphoreType.DMA((2,))],
+            )(*[pltpu.with_memory_space_constraint(v, pltpu.VMEM) for v in (state, weights)])
+        )
 
     in_specs = (
         P(None, "gx", "gy", "gz"),

time: 23.6 us -> 23.1 us (0.979)
  local copies, waits for them, and re-layouts: 1.23 us -> 0 us
  Pallas kernels: 21.6 us -> 22.3 us
    unnamed x2 -> x0, local copies, waits for them, and re-layouts: 1.23 us -> none
    pallas_call x0 -> x1, Pallas kernels: none -> 0.68 us  [local(): pl.pallas_call(store, out_shape=[jax.ShapeDtypeStruct((COMPS, X, Y, Z), j...]
where the time goes in v2:
time: 23.1 us; the launch traced here: 22.9 us
  Pallas kernels  22.3 us (97%)
  between operations  0.64 us (3%)
    pallas_call x1, Pallas kernels, local(): pl.pallas_call(functools.partial(kernel, sizes), out_shape=[pltpu.VMEM((C...  21.6 us
    pallas_call x1, Pallas kernels, local(): pl.pallas_call(store, out_shape=[jax.ShapeDtypeStruct((COMPS, X, Y, Z), j...  0.68 us

profile of v2, /device:TPU:0, one launch (start us, length us, event | category | flops | bytes accessed | tf_op | source)
XLA Modules:
  0.0 22.9 jit_solution(12342874943925821974)
XLA Ops:
  0.6 21.6 %shard_map.59 = (f32[9,4,8,128]{3,2,1,0:T(8,128)S(1)}, f32[1,2,32]{2,1,0:T(2,128)S(1)}) custom-call(f32[5,4,8,128]{3,2,1,0:T(8,128)} %sp_hbm.1, f32[3,4,8,128]{3,2,1,0:T(8,128)} %ve_hbm.1, f32[4,8,128]{2,1,0:T(8,128)} %pr_hbm.1, s32[3,1,2,32]{3,2,1,0:T(2,128)} %wa_hbm.1), custom_call_target="tpu_custom_call" | custom-call | tf_op jit(solution)/shard_map/pallas_call | solution.py:730
  22.2 0.7 %shard_map.60 = (f32[9,4,8,128]{3,2,1,0:T(8,128)}, f32[1,2,32]{2,1,0:T(2,128)}) custom-call(f32[9,4,8,128]{3,2,1,0:T(8,128)S(1)} %get-tuple-element.4.state, f32[1,2,32]{2,1,0:T(2,128)S(1)} %get-tuple-element.5.weights), custom_call_target="tpu_custom_call" | custom-call | tf_op jit(solution)/shard_map/pallas_call | solution.py:773

commit v3 on v2

--- a/solution.py
+++ b/solution.py
@@ -60,6 +60,15 @@
     return density, safe, inverse, velocity, pressure
 
 
+def state_of(density, momentum, energy):
+    safe = jnp.maximum(density, FLOOR)
+    inverse = 1.0 / safe
+    velocity = [m * inverse for m in momentum]
+    kinetic = momentum[0] * velocity[0] + momentum[1] * velocity[1] + momentum[2] * velocity[2]
+    pressure = (GAMMA - 1.0) * (energy - 0.5 * kinetic)
+    return safe, velocity, pressure
+
+
 def sound_of(inverse, pressure):
     return jnp.sqrt(GAMMA * jnp.maximum(pressure, FLOOR) * inverse)
 
@@ -88,8 +97,8 @@
 
 def kernel(
     sizes, sp_hbm, ve_hbm, pr_hbm, wa_hbm, out, bl, sp, ve, pr, wa, load_sem,
-    xsp, xve, xpr, ys, yr, hy, zs, zr, es, er, pk, pn, pz, qz,
-    dx, du, dw, lows, deltas, halo_send, halo_recv, near_sem, all_sem, *reduce_scratch
+    xsp, xve, xpr, ys, yr, hy, zs, zr, es, er, pk, pnx, pny, pz, qz,
+    dx, du, dw, lows, deltas, halo_send, halo_recv, near_sem, all_sem, relay, relay_send, relay_recv, *reduce_scratch
 ):
     X, Y, Z = pr.shape
     EX, EY, EZ = wa.shape[1:]
@@ -112,6 +121,10 @@
     def step(d, k):
         return tuple(k % sizes[d] if a == d else 0 for a in range(3))
 
+    relayed = len(groups) == 1
+    if relayed:
+        reduce_scratch[1][...] = jnp.zeros_like(reduce_scratch[1])
+
     def traced(flag):
         return jnp.where(flag, 1, 0).astype(jnp.int32)
 
@@ -183,8 +196,6 @@
 
     for copy in loads:
         copy.wait()
-
-    started = []
 
     def send(src, dst, slot, off):
         copy = pltpu.make_async_remote_copy(
@@ -198,6 +209,34 @@
         copy.start()
         started.append(copy)
         return copy
+
+    origin = (me[0] == 0) & (me[1] <= 1)
+    next_up = origin & (me[2] == 1)
+    origin = origin & (me[2] == 0)
+    plane_rows = ((origin, devices - 2), (jnp.logical_not(origin), devices - 3))
+    relay_copy = pltpu.make_async_remote_copy(
+        src_ref=reduce_scratch[0],
+        dst_ref=relay,
+        send_sem=relay_send,
+        recv_sem=relay_recv,
+        device_id=neighbour(2, 1),
+        device_id_type=MESH,
+    )
+
+    def speed_out():
+        await_all()
+        if not relayed:
+            spread_start(0, 0, speed_row)
+            return
+
+        @pl.when(next_up)
+        def _():
+            relay_copy.wait_recv()
+            spread_start(0, 0, jnp.maximum(speed_row, relay[...]))
+
+        @pl.when(jnp.logical_not(origin | next_up))
+        def _():
+            spread_start(0, 0, speed_row)
 
     def spread_copy(turn, stage, i):
         base = 4 * (turn * len(groups) + stage)
@@ -237,10 +276,10 @@
             def _(i=i):
                 buf[i : i + 1] = row
 
-    def spread_whole(turn, stage):
+    def spread_whole(turn, stage, rows=None):
         base = 4 * (turn * len(groups) + stage)
         _, buf, ssem, rsem = reduce_scratch[base : base + 4]
-        rows = buf.at[pl.ds(0, buf.shape[0] - 1)]
+        rows = buf.at[pl.ds(0, rows or buf.shape[0] - 1)]
         return pltpu.make_async_remote_copy(
             src_ref=rows,
             dst_ref=rows,
@@ -254,13 +293,27 @@
         for stage in range(len(groups)):
             if stage > 0:
                 spread_start(turn, stage, row)
-            spread_whole(turn, stage).wait_recv()
+            if turn == 0 and relayed:
+                for flag, rows in plane_rows:
+
+                    @pl.when(flag)
+                    def _(rows=rows):
+                        spread_whole(turn, stage, rows).wait_recv()
+            else:
+                spread_whole(turn, stage).wait_recv()
             row = combine(reduce_scratch[4 * (turn * len(groups) + stage) + 1][...])
         return row
 
     def spread_sent(turn):
         for stage in range(len(groups)):
-            spread_whole(turn, stage).wait_send()
+            if turn == 0 and relayed:
+
+                @pl.when(jnp.logical_not(origin))
+                def _():
+                    spread_whole(turn, stage).wait_send()
+
+            else:
+                spread_whole(turn, stage).wait_send()
 
     row_index = lax.broadcasted_iota(jnp.int32, (1, Y, Z), 1)
     lane_index = lax.broadcasted_iota(jnp.int32, (1, Y, Z), 2)
@@ -276,10 +329,19 @@
             value = op(value, jnp.where(low, roll(value, -s, axis), roll(value, s, axis)))
         return value
 
+    def lane_group(value, op):
+        place = lane_index & (P_SIZE - 1)
+        for s in range(1, P_SIZE):
+            ahead = roll(value, -s, 2)
+            behind = roll(value, P_SIZE - s, 2)
+            turned = jnp.where(place < P_SIZE - s, ahead, behind)
+            whole = turned if s == 1 else op(whole, turned)
+        return op(value, whole)
+
     def element(value, op):
         parts = value.reshape(EX, P_SIZE, Y, Z)
         value = op(op(parts[:, 0], parts[:, 1]), op(parts[:, 2], parts[:, 3]))
-        return mesh_group(mesh_group(value, 1, op), 2, op)
+        return lane_group(mesh_group(value, 1, op), op)
 
     def nodes(value):
         return jnp.broadcast_to(value[:, None], (EX, P_SIZE, Y, Z)).reshape(X, Y, Z)
@@ -300,6 +362,34 @@
             return ve[comp - SPECIES]
         return pr[...]
 
+    late = me[2] == corner[2]
+    ahead = late & (me[1] < corner[1] - 1)
+    last_x = me[0] == corner[0]
+    started = []
+    arrivals = {}
+
+    def halo(key, src, dst, slot, off):
+        copy = pltpu.make_async_remote_copy(
+            src_ref=src,
+            dst_ref=dst,
+            send_sem=halo_send.at[slot],
+            recv_sem=halo_recv.at[slot],
+            device_id=device(off),
+            device_id_type=MESH,
+        )
+        arrivals.setdefault(key, []).append(copy)
+        started.append(copy)
+
+    for side, k in ((0, 1), (1, -1)):
+        at = X - 2 if side == 0 else 0
+        halo(("x", side), sp.at[:, at : at + 2], xsp.at[side], 3 * side, step(0, k))
+        halo(("x", side), ve.at[:, at : at + 2], xve.at[side], 3 * side + 1, step(0, k))
+        halo(("x", side), pr.at[at : at + 2], xpr.at[side], 3 * side + 2, step(0, k))
+
+    @pl.when(ahead & last_x)
+    def _():
+        arrivals["x", 0][0].start()
+
     own_inputs = [block(c) for c in range(COMPS)]
 
     cons = conserved_of(own_inputs)
@@ -307,13 +397,11 @@
     sound = sound_of(inverse, pressure)
     speed = jnp.abs(velocity[0]) + jnp.abs(velocity[1]) + jnp.abs(velocity[2]) + 3.0 * sound
     speed_row = jnp.broadcast_to(total(speed, jnp.maximum), (1, ROW))
-    late = me[2] == corner[2]
     last_chip = (me[0] == corner[0]) & (me[1] >= corner[1] - 1) & late
 
     @pl.when(last_chip)
     def _():
-        await_all()
-        spread_start(0, 0, speed_row)
+        speed_out()
 
 
     for c in range(COMPS):
@@ -349,41 +437,40 @@
             flags = jnp.dot(flags, widen, preferred_element_type=jnp.float32)
             layers.append(jnp.dot(heighten, flags, preferred_element_type=jnp.float32)[None])
         walls.append(jnp.concatenate(layers, axis=0))
-        es[d, 0] = rho_min
-        es[d, 1] = p_min
-        es[d, 2] = walls[d]
-
-    arrivals = {}
-
-    def halo(key, src, dst, slot, off):
-        copy = pltpu.make_async_remote_copy(
-            src_ref=src,
-            dst_ref=dst,
-            send_sem=halo_send.at[slot],
-            recv_sem=halo_recv.at[slot],
-            device_id=device(off),
-            device_id_type=MESH,
-        )
-        arrivals.setdefault(key, []).append(copy)
-        started.append(copy)
+        turn_row = row_index & (P_SIZE - 1)
+        es[d] = jnp.where(turn_row == 0, rho_min, jnp.where(turn_row == 1, p_min, walls[d]))
+
+    def spread_rows(value, which):
+        value = jnp.where((row_index & (P_SIZE - 1)) == which, value, jnp.inf)
+        return mesh_group(value, 1, jnp.minimum)
+
+    def edge(side, d, which):
+        side = 0 if sizes[d] == 2 and d == 0 else side
+        return spread_rows(er[side, d], which)
 
     for side, k in ((0, 1), (1, -1)):
-        at = X - 2 if side == 0 else 0
-        halo(("x", side), sp.at[:, at : at + 2], xsp.at[side], 3 * side, step(0, k))
-        halo(("x", side), ve.at[:, at : at + 2], xve.at[side], 3 * side + 1, step(0, k))
-        halo(("x", side), pr.at[at : at + 2], xpr.at[side], 3 * side + 2, step(0, k))
         halo(("y", side), ys.at[side], yr.at[side], 6 + side, step(1, k))
         halo(("z", side), zs, zr.at[side], 8 + side, step(2, k))
         for d in range(3):
+            if d == 0 and sizes[0] == 2 and side == 1:
+                arrivals["e", d, side] = []
+                continue
             halo(("e", d, side), es.at[d], er.at[side, d], 10 + 2 * d + side, step(d, k))
 
-    def send_halo(d):
+    def send_halo(d, skip=0):
         for side, k in ((0, 1), (1, -1)):
-            if (d, k) in links:
+            if (d, k) in links and not skip:
                 await_near(d, k)
             for key in ((AXES[d][1], side), ("e", d, side)):
-                for copy in arrivals[key]:
+                for copy in arrivals[key][skip if side == 0 and key[0] != "e" else 0 :]:
                     copy.start()
+            if d == 2 and side == 0 and relayed:
+
+                @pl.when(origin)
+                def _():
+                    reduce_scratch[0][...] = speed_row
+                    relay_copy.start()
+
 
     @pl.when(jnp.logical_not(late))
     def _():
@@ -392,16 +479,26 @@
 
     send_halo(2)
 
+    @pl.when(ahead & jnp.logical_not(last_x))
+    def _():
+        for k in (1, -1):
+            if (0, k) in links:
+                await_near(0, k)
+        arrivals["x", 0][0].start()
+
     @pl.when(late)
     def _():
         send_halo(1)
 
     @pl.when(jnp.logical_not(last_chip))
     def _():
-        await_all()
-        spread_start(0, 0, speed_row)
-
-    @pl.when(late)
+        speed_out()
+
+    @pl.when(ahead)
+    def _():
+        send_halo(0, 1)
+
+    @pl.when(late & jnp.logical_not(ahead))
     def _():
         send_halo(0)
 
@@ -416,57 +513,60 @@
         _, _, h_inv, h_vel, h_p = primitives(halo)
         h_rate = jnp.abs(h_vel[d]) + sound_of(h_inv, h_p)
         rate = jnp.abs(velocity[d]) + sound
-        at_first, last = ix == 0, ix == n - 1
-        two_first, two_last = ix < 2, ix >= n - 2
-
-        def right_of(value, beyond):
-            return roll(jnp.where(at_first, beyond, value), -1, d)
-
+
+        def beside(value, beyond, k):
+            edge_of = ix < k if k > 0 else ix >= n + k
+            return roll(jnp.where(edge_of, beyond, value), -k, d)
+
+        shifts = (-2, -1, 1, 2)
+        along = {k: {d: beside(velocity[d], h_vel[d], k)} for k in shifts}
+        p_at = {k: beside(pressure, h_p, k) for k in shifts}
         arrive("e", d, 0)
         arrive("e", d, 1)
-        flag = right_of(walls[d], er[1, d, 2])
-        flag_low = roll(walls[d], -1, d)
-        ends = (ix & (P_SIZE - 1)) == P_SIZE - 1
-        wall = nodes(jnp.where(ends, flag, 0.0)) > 0.5
-        wall_low = nodes(jnp.where(ends, flag_low, 0.0)) > 0.5
-        half_rate = 0.5 * jnp.maximum(rate, right_of(rate, h_rate))
-        half_low = 0.5 * jnp.maximum(h_rate, roll(rate, -1, d))
-        wall_p = 0.5 * (pressure + right_of(pressure, h_p))
-        wall_p_low = 0.5 * (h_p + roll(pressure, -1, d))
+        flag = roll(jnp.where(ix == 0, edge(1, d, 2), walls[d]), -1, d)
+        ends = ix & (P_SIZE - 1)
+        wall = nodes(jnp.where(ends == P_SIZE - 1, flag, 0.0)) > 0.5
+        wall_low = nodes(jnp.where(ends == 0, walls[d], 0.0)) > 0.5
+        half_rate = 0.5 * jnp.maximum(rate, beside(rate, h_rate, 1))
+        half_low = 0.5 * jnp.maximum(beside(rate, h_rate, -1), rate)
+        wall_p = 0.5 * (pressure + p_at[1])
+        wall_p_low = 0.5 * (p_at[-1] + pressure)
         for c in range(COMPS):
+            u_at = {k: beside(cons[c], halo[c], k) for k in shifts}
+            f_at = {k: flux_term({c: u_at[k]}, along[k], p_at[k], c, d) for k in shifts}
             f = flux_term(cons, velocity, pressure, c, d)
-            h = flux_term(halo, h_vel, h_p, c, d)
             is_normal = c == SPECIES + d
             low, diff = face_pair(
-                roll(jnp.where(last, h, f), 1, d),
+                f_at[-1],
                 f,
-                right_of(f, h),
-                roll(jnp.where(two_first, h, f), -2, d),
-                right_of(cons[c], halo[c]) - cons[c],
+                f_at[1],
+                f_at[2],
+                u_at[1] - cons[c],
                 half_rate,
                 wall,
                 wall_p if is_normal else None,
             )
-            edge_low, edge_diff = face_pair(
-                roll(h, 1, d),
-                h,
-                roll(f, -1, d),
-                roll(f, -2, d),
-                roll(cons[c], -1, d) - halo[c],
+            before_low, before_diff = face_pair(
+                f_at[-2],
+                f_at[-1],
+                f,
+                f_at[1],
+                cons[c] - u_at[-1],
                 half_low,
                 wall_low,
                 wall_p_low if is_normal else None,
             )
-            before_low = roll(jnp.where(last, edge_low, low), 1, d)
-            before_diff = roll(jnp.where(last, edge_diff, diff), 1, d)
             du[number, c] = diff
             dw[number, c] = before_diff
+            slot = max(c - SPECIES + 1, 0)
             if first:
                 lows[c] = low - before_low
-                deltas[c] = diff - before_diff
             else:
                 lows[c] += low - before_low
-                deltas[c] += diff - before_diff
+            if first and c in (0, *range(SPECIES, COMPS)):
+                deltas[slot] = diff - before_diff
+            else:
+                deltas[slot] += diff - before_diff
 
     arrive("y", 0)
     arrive("y", 1)
@@ -515,7 +615,7 @@
         if (x + 1) % P_SIZE:
             planes.append(jnp.zeros((1, Y, Z), jnp.float32))
         elif x == X - 1:
-            planes.append(er[1, 0, 2, 0:1])
+            planes.append(edge(1, 0, 2)[0:1])
         else:
             e = (x + 1) // P_SIZE
             planes.append(walls[0][e : e + 1])
@@ -539,30 +639,38 @@
         )
         dx[c] = diff
         lows[c] += low[1:] - low[:-1]
-        deltas[c] += diff[1:] - diff[:-1]
+        deltas[max(c - SPECIES + 1, 0)] += diff[1:] - diff[:-1]
 
     def bound(own, which):
         best = own
         for d in (1, 2):
             n = extent[d]
-            up = jnp.where(index[d] < P_SIZE, er[1, d, which], own)
-            down = jnp.where(index[d] >= n - P_SIZE, er[0, d, which], own)
+            up = jnp.where(index[d] < P_SIZE, edge(1, d, which), own)
+            down = jnp.where(index[d] >= n - P_SIZE, edge(0, d, which), own)
             best = jnp.minimum(best, jnp.minimum(roll(up, -P_SIZE, d), roll(down, P_SIZE, d)))
-        chain = joined(er[0, 0, which, EX - 1 : EX], own, er[1, 0, which, 0:1])
+        chain = joined(edge(0, 0, which)[EX - 1 : EX], own, edge(1, 0, which)[0:1])
         return jnp.minimum(best, jnp.minimum(chain[:EX], chain[2:]))
 
     rho_bound = bound(rho_min, 0)
     p_bound = bound(p_min, 1)
 
+    fluxes = [sum([lows[c] for c in range(1, SPECIES)], lows[0])]
+    fluxes += [lows[c] for c in range(SPECIES, COMPS)]
+    jumps = [deltas[i] for i in range(COMPS - SPECIES + 1)]
+
     speed_max = spread_end(0, lambda rows: jnp.max(rows, axis=0, keepdims=True))
-    ratio = (COURANT / speed_max)[0:1, 0:1].reshape(1, 1, 1)
-
-    for c in range(COMPS):
-        lows[c] = cons[c] - ratio * lows[c]
-        deltas[c] = -(ratio * deltas[c])
-    low_density, low_safe, _, _, low_pressure = primitives([lows[c] for c in range(COMPS)])
-    low_sigma = entropy(low_density, low_safe, low_pressure)
-    d_rho = sum([deltas[c] for c in range(1, SPECIES)], deltas[0])
+    ratio = (COURANT / speed_max).reshape(1, 1, ROW)
+
+    def five(values):
+        return [sum([values[c] for c in range(1, SPECIES)], values[0])] + [
+            values[c] for c in range(SPECIES, COMPS)
+        ]
+
+    low_five = [u - ratio * f for u, f in zip(five(cons), fluxes)]
+    d_five = [-(ratio * d) for d in jumps]
+    low_safe, _, low_pressure = state_of(low_five[0], low_five[1:4], low_five[4])
+    low_sigma = entropy(low_five[0], low_safe, low_pressure)
+    d_rho = d_five[0]
     rho_scale = 1.0 / jnp.maximum(-d_rho, SLOPE_FLOOR)
     count = X * Y * Z * sizes[0] * sizes[1] * sizes[2]
     stat_lane = lax.broadcasted_iota(jnp.int32, (1, ROW), 1)
@@ -574,11 +682,15 @@
             jnp.sum(rows, axis=0, keepdims=True),
         )
 
-    def next_blend(got, packed):
-        t_density, rho_scale, t_p, p_scale, rho_bound, p_bound, mean_square, base = packed
+    def broadcast_stats(got):
         lowest_rho = got[0:1, 0:1].reshape(1, 1, 1)
         lowest_p = got[0:1, 1:2].reshape(1, 1, 1)
         spread = got[0:1, 2:3].reshape(1, 1, 1) * (1.0 / count) + SPREAD
+        return lowest_rho, lowest_p, spread
+
+    def next_blend(got, packed):
+        t_density, rho_scale, t_p, p_scale, rho_bound, p_bound, mean_square, base = packed
+        lowest_rho, lowest_p, spread = got
         rho_target = rho_bound - RELAX * jnp.maximum(rho_bound - lowest_rho, 0.0)
         p_target = p_bound - RELAX * jnp.maximum(p_bound - lowest_p, 0.0)
         step_rho = jnp.minimum(t_density - nodes(rho_target), 0.0) * rho_scale
@@ -588,14 +700,59 @@
         return jnp.maximum(jnp.minimum(cap, base + lowered), 0.0)
 
     per_edge = Z // (2 * P_SIZE)
+    depth = 2 * X + 2 * EX
+
+    def share(phase, fields):
+        at = 0
+        for value in fields:
+            pk[phase, at : at + value.shape[0]] = value
+            at += value.shape[0]
+        slot = 16 + 6 * phase
+        for side, k in ((0, 1), (1, -1)):
+            if side == 0 or sizes[0] > 2:
+                arrivals["b", phase, 0, side] = [
+                    send(pk.at[phase], pnx.at[side, phase], slot + side, step(0, k))
+                ]
+            else:
+                arrivals["b", phase, 0, side] = []
+        for side, k in ((0, 1), (1, -1)):
+            rows = pl.ds(Y - P_SIZE, P_SIZE) if side == 0 else pl.ds(0, P_SIZE)
+            arrivals["b", phase, 1, side] = [
+                send(pk.at[phase, :, rows], pny.at[phase, :, rows], slot + 2 + side, step(1, k))
+            ]
+        items = [value[x : x + 1] for value in fields for x in range(value.shape[0])]
+        for v in range(pz.shape[1]):
+            packed = jnp.zeros((1, Y, Z), jnp.float32)
+            for j, item in enumerate(items[v * per_edge : (v + 1) * per_edge]):
+                at = 2 * P_SIZE * j
+                moved = roll(item, at + P_SIZE, 2)
+                inside = (lane_index >= at) & (lane_index < at + 2 * P_SIZE)
+                packed = jnp.where(inside, moved, packed)
+            pz[phase, v] = packed[0]
+        for side, k in ((0, 1), (1, -1)):
+            arrivals["b", phase, 2, side] = [
+                send(pz.at[phase], qz.at[side, phase], slot + 4 + side, step(2, k))
+            ]
+
+    def unpack(early, late):
+        low_density, d_density, rho_bound, p_bound = early
+        t_p, p_scale, mean_square, base = late
+        t_density = low_density + nodes(base) * d_density
+        scale = 1.0 / jnp.maximum(-d_density, SLOPE_FLOOR)
+        return t_density, scale, t_p, p_scale, rho_bound, p_bound, mean_square, base
+
+    def cut_fields(layer):
+        ends = (0, X, 2 * X, 2 * X + EX, depth)
+        return [layer(a, b) for a, b in zip(ends[:-1], ends[1:])]
+
     blend = None
     for newton in range(ITERS):
         blend_nodes = None if blend is None else nodes(blend)
         trial = [
-            lows[c] + (deltas[c] if blend is None else blend_nodes * deltas[c])
-            for c in range(COMPS)
+            low + (d if blend is None else blend_nodes * d) for low, d in zip(low_five, d_five)
         ]
-        t_density, t_safe, _, t_vel, t_p = primitives(trial)
+        t_density = trial[0]
+        t_safe, t_vel, t_p = state_of(t_density, trial[1:4], trial[4])
         residual = entropy(t_density, t_safe, t_p) - low_sigma
         square = residual * residual
         stats = jnp.where(
@@ -604,66 +761,78 @@
             jnp.where(stat_lane == 1, total(t_p, jnp.minimum), total(square, jnp.add)),
         )
         spread_start(newton + 1, 0, stats)
-        cross = sum([t_vel[k] * deltas[SPECIES + k] for k in range(1, 3)], t_vel[0] * deltas[SPECIES])
+        if newton == ITERS - 2:
+            share(0, (low_five[0], d_rho, rho_bound, p_bound))
+        cross = t_vel[0] * d_five[1] + t_vel[1] * d_five[2] + t_vel[2] * d_five[3]
         speed2 = t_vel[0] * t_vel[0] + t_vel[1] * t_vel[1] + t_vel[2] * t_vel[2]
-        slope = (GAMMA - 1.0) * (deltas[SPECIES + 3] - cross + 0.5 * speed2 * d_rho)
+        slope = (GAMMA - 1.0) * (d_five[4] - cross + 0.5 * speed2 * d_rho)
         p_scale = 1.0 / jnp.maximum(-slope, SLOPE_FLOOR)
         mean_square = element(square, jnp.add) * (1.0 / (P_SIZE**3))
         base = jnp.ones((EX, Y, Z), jnp.float32) if blend is None else blend
+        beside = {}
         if newton == ITERS - 1:
-            fields = (t_density, rho_scale, t_p, p_scale)
-            for i, value in enumerate(fields):
-                pk[i * X : (i + 1) * X] = value
-            for i, value in enumerate((rho_bound, p_bound, mean_square, base)):
-                pk[4 * X + i * EX : 4 * X + (i + 1) * EX] = value
-            items = [value[x : x + 1] for value in fields for x in range(X)]
-            for value in (rho_bound, p_bound, mean_square, base):
-                items += [value[e : e + 1] for e in range(EX)]
-            for v in range(pz.shape[0]):
-                packed = jnp.zeros((1, Y, Z), jnp.float32)
-                for j, item in enumerate(items[v * per_edge : (v + 1) * per_edge]):
-                    at = 2 * P_SIZE * j
-                    moved = roll(item, at + P_SIZE, 2)
-                    inside = (lane_index >= at) & (lane_index < at + 2 * P_SIZE)
-                    packed = jnp.where(inside, moved, packed)
-                pz[v] = packed[0]
-            for side, k in ((0, 1), (1, -1)):
-                arrivals["b", 2, side] = [send(pz, qz.at[side], 20 + side, step(2, k))]
-            for d in (0, 1):
-                for side, k in ((0, 1), (1, -1)):
-                    if side == 0 or sizes[d] > 2:
-                        copy = send(pk, pn.at[side, d], 16 + 2 * d + side, step(d, k))
-                        arrivals["b", d, side] = [copy]
-                    else:
-                        arrivals["b", d, side] = []
-        got = spread_end(newton + 1, combine_stats)
+            share(1, (t_p, p_scale, mean_square, base))
+            for copy in started:
+                copy.wait_send()
+            for turn in range(ITERS):
+                spread_sent(turn)
+            if relayed:
+
+                @pl.when(origin)
+                def _():
+                    relay_copy.wait_send()
+
+            def arrive_both(d):
+                for phase in (0, 1):
+                    for side in (0, 1):
+                        arrive("b", phase, d, side)
+
+            arrive_both(1)
+            arrive_both(2)
+            beside[1] = unpack(
+                *[cut_fields(lambda a, b: pny[phase, a:b]) for phase in (0, 1)]
+            )
+            near = (lane_index & (2 * P_SIZE - 1)) < P_SIZE
+            halves = []
+            for phase in (0, 1):
+                edges = [
+                    jnp.where(near, qz[0, phase, v][None], qz[1, phase, v][None])
+                    for v in range(pz.shape[1])
+                ]
+                items = [
+                    roll(edges[j // per_edge], -(2 * P_SIZE * (j % per_edge) + P_SIZE), 2)
+                    for j in range(depth)
+                ]
+                halves.append(cut_fields(lambda a, b: jnp.concatenate(items[a:b], axis=0)))
+            beside[2] = unpack(*halves)
+            arrive_both(0)
+            for side in (0, 1):
+                if side == 0 or sizes[0] > 2:
+                    beside[0, side] = unpack(
+                        *[cut_fields(lambda a, b: pnx[side, phase, a:b]) for phase in (0, 1)]
+                    )
+        got = broadcast_stats(spread_end(newton + 1, combine_stats))
         blend = next_blend(
             got, (t_density, rho_scale, t_p, p_scale, rho_bound, p_bound, mean_square, base)
         )
 
-    beside = {}
-    arrive("b", 2, 0)
-    arrive("b", 2, 1)
-    near = (lane_index & (2 * P_SIZE - 1)) < P_SIZE
-    edges = [jnp.where(near, qz[0, v][None], qz[1, v][None]) for v in range(qz.shape[1])]
-    items = [
-        roll(edges[j // per_edge], -(2 * P_SIZE * (j % per_edge) + P_SIZE), 2)
-        for j in range(4 * X + 4 * EX)
-    ]
-    packed = [jnp.concatenate(items[i * X : (i + 1) * X], axis=0) for i in range(4)]
-    packed += [
-        jnp.concatenate(items[4 * X + i * EX : 4 * X + (i + 1) * EX], axis=0) for i in range(4)
-    ]
-    beside[2, 0] = beside[2, 1] = next_blend(got, packed)
-    for d in (0, 1):
-        for side in (0, 1):
-            arrive("b", d, side)
-            if side == 1 and sizes[d] == 2:
-                beside[d, side] = beside[d, 0]
-                continue
-            packed = [pn[side, d, i * X : (i + 1) * X] for i in range(4)]
-            packed += [pn[side, d, 4 * X + i * EX : 4 * X + (i + 1) * EX] for i in range(4)]
-            beside[d, side] = next_blend(got, packed)
+    beside = {key: next_blend(got, packed) for key, packed in beside.items()}
+    beside.setdefault((0, 1), beside[0, 0])
+
+    theta = []
+    for d in (2, 1):
+        above = roll(jnp.where(index[d] == 0, beside[d], blend), -1, d)
+        below = roll(jnp.where(index[d] == extent[d] - 1, beside[d], blend), 1, d)
+        theta.append((nodes(jnp.minimum(blend, above)), nodes(jnp.minimum(blend, below))))
+    x_blend = joined(beside[0, 0][EX - 1 : EX], nodes(blend), beside[0, 1][0:1])
+    x_theta = jnp.minimum(x_blend[:-1], x_blend[1:])
+    for c in range(COMPS):
+        faces = x_theta * dx[c]
+        change = lows[c] + (faces[1:] - faces[:-1])
+        for number in range(2):
+            upper, lower = theta[number]
+            change += upper * du[number, c] - lower * dw[number, c]
+        out[c] = cons[c] - ratio * change
 
     pick_lanes = (
         lax.broadcasted_iota(jnp.int32, (Z, EZ), 1) * P_SIZE
@@ -675,25 +844,7 @@
         )
         bl[e] = jnp.concatenate([few[j * P_SIZE : j * P_SIZE + 1] for j in range(EY)], axis=0)
 
-    theta = []
-    for d in (2, 1):
-        above = roll(jnp.where(index[d] == 0, beside[d, 1], blend), -1, d)
-        below = roll(jnp.where(index[d] == extent[d] - 1, beside[d, 0], blend), 1, d)
-        theta.append((nodes(jnp.minimum(blend, above)), nodes(jnp.minimum(blend, below))))
-    x_blend = joined(beside[0, 0][EX - 1 : EX], nodes(blend), beside[0, 1][0:1])
-    x_theta = jnp.minimum(x_blend[:-1], x_blend[1:])
-    for c in range(COMPS):
-        faces = x_theta * dx[c]
-        change = faces[1:] - faces[:-1]
-        for number in range(2):
-            upper, lower = theta[number]
-            change += upper * du[number, c] - lower * dw[number, c]
-        out[c] = lows[c] - ratio * change
-
-    for copy in started:
-        copy.wait_send()
-    for turn in range(ITERS + 1):
-        spread_sent(turn)
+    spread_sent(ITERS)
 
 
 def store(state, weights, state_hbm, weights_hbm, sem):
@@ -714,7 +865,8 @@
         X, Y, Z = pressure_in.shape
         EX, EY, EZ = wall_types.shape[1:]
         packs = -(-COMPS // (Z // (4 * X)))
-        edge_packs = -(-(4 * X + 4 * EX) // (Z // (2 * P_SIZE)))
+        depth = 2 * X + 2 * EX
+        edge_packs = -(-depth // (Z // (2 * P_SIZE)))
         vmem = lambda *shape: pltpu.VMEM(shape, jnp.float32)
         reduce_scratch = []
         for _ in range(ITERS + 1):
@@ -749,21 +901,25 @@
                     vmem(COMPS, X, Y, Z),
                     vmem(packs, Y, Z),
                     vmem(2, packs, Y, Z),
-                    vmem(3, 3, EX, Y, Z),
-                    vmem(2, 3, 3, EX, Y, Z),
-                    vmem(4 * X + 4 * EX, Y, Z),
-                    vmem(2, 2, 4 * X + 4 * EX, Y, Z),
-                    vmem(edge_packs, Y, Z),
+                    vmem(3, EX, Y, Z),
+                    vmem(2, 3, EX, Y, Z),
+                    vmem(2, depth, Y, Z),
+                    vmem(2, 2, depth, Y, Z),
+                    vmem(2, depth, Y, Z),
                     vmem(2, edge_packs, Y, Z),
+                    vmem(2, 2, edge_packs, Y, Z),
                     vmem(COMPS, X + 1, Y, Z),
                     vmem(2, COMPS, X, Y, Z),
                     vmem(2, COMPS, X, Y, Z),
                     vmem(COMPS, X, Y, Z),
-                    vmem(COMPS, X, Y, Z),
-                    pltpu.SemaphoreType.DMA((22,)),
-                    pltpu.SemaphoreType.DMA((22,)),
+                    vmem(COMPS - SPECIES + 1, X, Y, Z),
+                    pltpu.SemaphoreType.DMA((28,)),
+                    pltpu.SemaphoreType.DMA((28,)),
                     pltpu.SemaphoreType.REGULAR((len(halo_links(sizes)),)),
                     pltpu.SemaphoreType.REGULAR,
+                    vmem(1, ROW),
+                    pltpu.SemaphoreType.DMA(()),
+                    pltpu.SemaphoreType.DMA(()),
                 ]
                 + reduce_scratch,
                 compiler_params=pltpu.CompilerParams(collective_id=0, has_side_effects=True),

time: 23.1 us -> 21.7 us (0.939)
  Pallas kernels: 22.3 us -> 20.9 us
    pallas_call x1, Pallas kernels: 21.6 us -> 20.3 us  [local(): pl.pallas_call(functools.partial(kernel, sizes), out_shape=[pltpu.VMEM((C...]
where the time goes in v3:
time: 21.7 us; the launch traced here: 21.6 us
  Pallas kernels  20.9 us (96%)
  between operations  0.64 us (3%)
    pallas_call x1, Pallas kernels, local(): pl.pallas_call(functools.partial(kernel, sizes), out_shape=[pltpu.VMEM((C...  20.3 us
    pallas_call x1, Pallas kernels, local(): pl.pallas_call(store, out_shape=[jax.ShapeDtypeStruct((COMPS, X, Y, Z), j...  0.68 us

profile of v3, /device:TPU:0, one launch (start us, length us, event | category | flops | bytes accessed | tf_op | source)
XLA Modules:
  0.0 21.6 jit_solution(1748274842710839343)
XLA Ops:
  0.6 20.3 %shard_map.59 = (f32[9,4,8,128]{3,2,1,0:T(8,128)S(1)}, f32[1,2,32]{2,1,0:T(2,128)S(1)}) custom-call(f32[5,4,8,128]{3,2,1,0:T(8,128)} %sp_hbm.1, f32[3,4,8,128]{3,2,1,0:T(8,128)} %ve_hbm.1, f32[4,8,128]{2,1,0:T(8,128)} %pr_hbm.1, s32[3,1,2,32]{3,2,1,0:T(2,128)} %wa_hbm.1), custom_call_target="tpu_custom_call" | custom-call | tf_op jit(solution)/shard_map/pallas_call | solution.py:882
  20.9 0.7 %shard_map.60 = (f32[9,4,8,128]{3,2,1,0:T(8,128)}, f32[1,2,32]{2,1,0:T(2,128)}) custom-call(f32[9,4,8,128]{3,2,1,0:T(8,128)S(1)} %get-tuple-element.4.state, f32[1,2,32]{2,1,0:T(2,128)S(1)} %get-tuple-element.5.weights), custom_call_target="tpu_custom_call" | custom-call | tf_op jit(solution)/shard_map/pallas_call | solution.py:929

commit v4 on v3

--- a/solution.py
+++ b/solution.py
@@ -96,17 +96,17 @@
 
 
 def kernel(
-    sizes, sp_hbm, ve_hbm, pr_hbm, wa_hbm, out, bl, sp, ve, pr, wa, load_sem,
-    xsp, xve, xpr, ys, yr, hy, zs, zr, es, er, pk, pnx, pny, pz, qz,
-    dx, du, dw, lows, deltas, halo_send, halo_recv, near_sem, all_sem, relay, relay_send, relay_recv, *reduce_scratch
+    sizes, sp_hbm, ve_hbm, pr_hbm, wa_hbm, out, bl, inp, wa, load_sem,
+    xh, ys, yr, hy, zs, zr, es, er, pk, pnx, pny, pz, qz, dx, du, dw, lows, deltas,
+    sent_sem, came_sem, near_sem, all_sem, relay, relay_sem, row_sent, row_came, *rows_scratch
 ):
-    X, Y, Z = pr.shape
+    X, Y, Z = inp.shape[1:]
     EX, EY, EZ = wa.shape[1:]
     loads = [
-        pltpu.make_async_copy(source, target, load_sem.at[i])
-        for i, (source, target) in enumerate(
-            ((sp_hbm, sp), (ve_hbm, ve), (pr_hbm, pr), (wa_hbm, wa))
-        )
+        pltpu.make_async_copy(sp_hbm, inp.at[:SPECIES], load_sem.at[0]),
+        pltpu.make_async_copy(ve_hbm, inp.at[SPECIES : SPECIES + 3], load_sem.at[0]),
+        pltpu.make_async_copy(pr_hbm, inp.at[SPECIES + 3], load_sem.at[0]),
+        pltpu.make_async_copy(wa_hbm, wa, load_sem.at[1]),
     ]
     for copy in loads:
         copy.start()
@@ -123,7 +123,7 @@
 
     relayed = len(groups) == 1
     if relayed:
-        reduce_scratch[1][...] = jnp.zeros_like(reduce_scratch[1])
+        rows_scratch[1][...] = jnp.zeros_like(rows_scratch[1])
 
     def traced(flag):
         return jnp.where(flag, 1, 0).astype(jnp.int32)
@@ -194,34 +194,21 @@
         def _():
             pl.semaphore_wait(all_sem, 1)
 
-    for copy in loads:
-        copy.wait()
-
-    def send(src, dst, slot, off):
-        copy = pltpu.make_async_remote_copy(
-            src_ref=src,
-            dst_ref=dst,
-            send_sem=halo_send.at[slot],
-            recv_sem=halo_recv.at[slot],
-            device_id=device(off),
-            device_id_type=MESH,
-        )
-        copy.start()
-        started.append(copy)
-        return copy
+    pltpu.make_async_copy(inp, inp, load_sem.at[0]).wait()
 
     origin = (me[0] == 0) & (me[1] <= 1)
     next_up = origin & (me[2] == 1)
     origin = origin & (me[2] == 0)
     plane_rows = ((origin, devices - 2), (jnp.logical_not(origin), devices - 3))
-    relay_copy = pltpu.make_async_remote_copy(
-        src_ref=reduce_scratch[0],
-        dst_ref=relay,
-        send_sem=relay_send,
-        recv_sem=relay_recv,
-        device_id=neighbour(2, 1),
-        device_id_type=MESH,
-    )
+    if relayed:
+        relay_copy = pltpu.make_async_remote_copy(
+            src_ref=rows_scratch[0],
+            dst_ref=relay,
+            send_sem=row_sent,
+            recv_sem=relay_sem,
+            device_id=neighbour(2, 1),
+            device_id_type=MESH,
+        )
 
     def speed_out():
         await_all()
@@ -238,9 +225,13 @@
         def _():
             spread_start(0, 0, speed_row)
 
+    def row_parts(turn, stage):
+        base = 2 * (turn * len(groups) + stage)
+        mine, buf = rows_scratch[base : base + 2]
+        return mine, buf, row_came.at[turn % 2 * len(groups) + stage]
+
     def spread_copy(turn, stage, i):
-        base = 4 * (turn * len(groups) + stage)
-        mine, buf, ssem, rsem = reduce_scratch[base : base + 4]
+        mine, buf, came = row_parts(turn, stage)
         group = groups[stage]
         off = group_offsets(sizes, group)[i]
         there = tuple(
@@ -251,16 +242,18 @@
         copy = pltpu.make_async_remote_copy(
             src_ref=mine,
             dst_ref=buf.at[pl.ds(i, 1)],
-            send_sem=ssem,
-            recv_sem=rsem,
+            send_sem=row_sent,
+            recv_sem=came,
             device_id=there,
             device_id_type=MESH,
         )
         return copy, can_be_me, functools.reduce(lambda a, b: a & b, [t == m for t, m in zip(there, me)])
 
     def spread_start(turn, stage, row):
-        base = 4 * (turn * len(groups) + stage)
-        mine, buf = reduce_scratch[base : base + 2]
+        if turn or stage:
+            before = turn * len(groups) + stage - 1
+            spread_sent(before // len(groups), before % len(groups))
+        mine, buf, _ = row_parts(turn, stage)
         mine[...] = row
         for i in range(buf.shape[0]):
             copy, can_be_me, is_me = spread_copy(turn, stage, i)
@@ -277,14 +270,13 @@
                 buf[i : i + 1] = row
 
     def spread_whole(turn, stage, rows=None):
-        base = 4 * (turn * len(groups) + stage)
-        _, buf, ssem, rsem = reduce_scratch[base : base + 4]
+        _, buf, came = row_parts(turn, stage)
         rows = buf.at[pl.ds(0, rows or buf.shape[0] - 1)]
         return pltpu.make_async_remote_copy(
             src_ref=rows,
             dst_ref=rows,
-            send_sem=ssem,
-            recv_sem=rsem,
+            send_sem=row_sent,
+            recv_sem=came,
             device_id=device((1, 1, 1)),
             device_id_type=MESH,
         )
@@ -301,19 +293,22 @@
                         spread_whole(turn, stage, rows).wait_recv()
             else:
                 spread_whole(turn, stage).wait_recv()
-            row = combine(reduce_scratch[4 * (turn * len(groups) + stage) + 1][...])
+            row = combine(row_parts(turn, stage)[1][...])
         return row
 
-    def spread_sent(turn):
-        for stage in range(len(groups)):
-            if turn == 0 and relayed:
-
-                @pl.when(jnp.logical_not(origin))
-                def _():
-                    spread_whole(turn, stage).wait_send()
-
-            else:
+    def spread_sent(turn, stage):
+        if turn == 0 and relayed:
+
+            @pl.when(jnp.logical_not(origin))
+            def _():
                 spread_whole(turn, stage).wait_send()
+
+            @pl.when(origin)
+            def _():
+                relay_copy.wait_send()
+
+        else:
+            spread_whole(turn, stage).wait_send()
 
     row_index = lax.broadcasted_iota(jnp.int32, (1, Y, Z), 1)
     lane_index = lax.broadcasted_iota(jnp.int32, (1, Y, Z), 2)
@@ -355,60 +350,95 @@
             value, axis=1, keepdims=True
         )
 
-    def block(comp):
-        if comp < SPECIES:
-            return sp[comp]
-        if comp < SPECIES + 3:
-            return ve[comp - SPECIES]
-        return pr[...]
-
     late = me[2] == corner[2]
-    ahead = late & (me[1] < corner[1] - 1)
     last_x = me[0] == corner[0]
-    started = []
-    arrivals = {}
-
-    def halo(key, src, dst, slot, off):
-        copy = pltpu.make_async_remote_copy(
+    last_chip = last_x & (me[1] >= corner[1] - 1) & late
+    first_sides = ((0, 1),) if sizes[0] == 2 else ((0, 1), (1, -1))
+    packs = zs.shape[0] - EX
+    body = COMPS * 2 * X
+
+    def remote(src, dst, sent, came, off):
+        return pltpu.make_async_remote_copy(
             src_ref=src,
             dst_ref=dst,
-            send_sem=halo_send.at[slot],
-            recv_sem=halo_recv.at[slot],
+            send_sem=sent_sem.at[sent],
+            recv_sem=came_sem.at[came],
             device_id=device(off),
             device_id_type=MESH,
         )
-        arrivals.setdefault(key, []).append(copy)
-        started.append(copy)
-
-    for side, k in ((0, 1), (1, -1)):
-        at = X - 2 if side == 0 else 0
-        halo(("x", side), sp.at[:, at : at + 2], xsp.at[side], 3 * side, step(0, k))
-        halo(("x", side), ve.at[:, at : at + 2], xve.at[side], 3 * side + 1, step(0, k))
-        halo(("x", side), pr.at[at : at + 2], xpr.at[side], 3 * side + 2, step(0, k))
-
-    @pl.when(ahead & last_x)
+
+    landing = {
+        "x": (xh, 0, 0),
+        "y": (yr, 1, 1),
+        "z": (zr, 2, 2),
+        "e": (er, 3, 3),
+        ("b", 0): (pnx, 0, 4),
+        ("b", 1): (pny.at[:, :, pl.ds(0, 2 * P_SIZE)], 1, 5),
+        ("b", 2): (qz, 2, 6),
+    }
+
+    def whole(key):
+        ref, sent, came = landing[key]
+        return remote(ref, ref, sent, came, step(2, 1))
+
+    def arrive(key):
+        whole(key).wait_recv()
+
+    def sent_all(key):
+        whole(key).wait_send()
+
+    def send_x():
+        for d, k in links:
+            if d == 0:
+                await_near(d, k)
+        for side, k in ((0, 1), (1, -1)):
+            at = X - 2 if side == 0 else 0
+            remote(inp.at[:, at : at + 2], xh.at[side], 0, 0, step(0, k)).start()
+
+    def send_e():
+        for side, k in first_sides:
+            remote(es, er.at[side], 3, 3, step(0, k)).start()
+
+    def send_y():
+        for side, k in ((0, 1), (1, -1)):
+            if (1, k) in links:
+                await_near(1, k)
+            remote(ys.at[side], yr.at[side], 1, 1, step(1, k)).start()
+
+    def send_z():
+        for side, k in ((0, 1), (1, -1)):
+            if (2, k) in links:
+                await_near(2, k)
+            remote(zs, zr.at[side], 2, 2, step(2, k)).start()
+            if side == 0 and relayed:
+
+                @pl.when(origin)
+                def _():
+                    rows_scratch[0][...] = speed_row
+                    relay_copy.start()
+
+    @pl.when(late & last_x & jnp.logical_not(last_chip))
     def _():
-        arrivals["x", 0][0].start()
-
-    own_inputs = [block(c) for c in range(COMPS)]
+        send_x()
+
+    own_inputs = [inp[c] for c in range(COMPS)]
 
     cons = conserved_of(own_inputs)
     density, _, inverse, velocity, pressure = primitives(cons)
     sound = sound_of(inverse, pressure)
     speed = jnp.abs(velocity[0]) + jnp.abs(velocity[1]) + jnp.abs(velocity[2]) + 3.0 * sound
     speed_row = jnp.broadcast_to(total(speed, jnp.maximum), (1, ROW))
-    last_chip = (me[0] == corner[0]) & (me[1] >= corner[1] - 1) & late
 
     @pl.when(last_chip)
     def _():
         speed_out()
-
+        send_x()
 
     for c in range(COMPS):
         for x in range(X):
-            ys[0, c, 2 * x : 2 * x + 2, :] = own_inputs[c][x, Y - 2 : Y, :]
-            ys[1, c, 2 * x : 2 * x + 2, :] = own_inputs[c][x, 0:2, :]
-    packs = zs.shape[0]
+            at = 2 * (c * X + x)
+            ys[0, at : at + 2, :] = own_inputs[c][x, Y - 2 : Y, :]
+            ys[1, at : at + 2, :] = own_inputs[c][x, 0:2, :]
     per_pack = Z // (4 * X)
     for v in range(packs):
         packed = jnp.zeros((1, Y, Z), jnp.float32)
@@ -429,6 +459,7 @@
         lax.broadcasted_iota(jnp.int32, (Y, EY), 0) // P_SIZE
         == lax.broadcasted_iota(jnp.int32, (Y, EY), 1)
     ).astype(jnp.float32)
+    loads[3].wait()
     walls = []
     for d in range(3):
         layers = []
@@ -438,73 +469,48 @@
             layers.append(jnp.dot(heighten, flags, preferred_element_type=jnp.float32)[None])
         walls.append(jnp.concatenate(layers, axis=0))
         turn_row = row_index & (P_SIZE - 1)
-        es[d] = jnp.where(turn_row == 0, rho_min, jnp.where(turn_row == 1, p_min, walls[d]))
+        fields = jnp.where(turn_row == 0, rho_min, jnp.where(turn_row == 1, p_min, walls[d]))
+        if d == 0:
+            es[...] = fields
+        elif d == 1:
+            for side in (0, 1):
+                ys[side, body : body + EX * Y, :] = fields.reshape(EX * Y, Z)
+        else:
+            zs[packs : packs + EX] = fields
 
     def spread_rows(value, which):
         value = jnp.where((row_index & (P_SIZE - 1)) == which, value, jnp.inf)
         return mesh_group(value, 1, jnp.minimum)
 
     def edge(side, d, which):
-        side = 0 if sizes[d] == 2 and d == 0 else side
-        return spread_rows(er[side, d], which)
-
-    for side, k in ((0, 1), (1, -1)):
-        halo(("y", side), ys.at[side], yr.at[side], 6 + side, step(1, k))
-        halo(("z", side), zs, zr.at[side], 8 + side, step(2, k))
-        for d in range(3):
-            if d == 0 and sizes[0] == 2 and side == 1:
-                arrivals["e", d, side] = []
-                continue
-            halo(("e", d, side), es.at[d], er.at[side, d], 10 + 2 * d + side, step(d, k))
-
-    def send_halo(d, skip=0):
-        for side, k in ((0, 1), (1, -1)):
-            if (d, k) in links and not skip:
-                await_near(d, k)
-            for key in ((AXES[d][1], side), ("e", d, side)):
-                for copy in arrivals[key][skip if side == 0 and key[0] != "e" else 0 :]:
-                    copy.start()
-            if d == 2 and side == 0 and relayed:
-
-                @pl.when(origin)
-                def _():
-                    reduce_scratch[0][...] = speed_row
-                    relay_copy.start()
-
+        if d == 0:
+            fields = er[0 if sizes[0] == 2 else side]
+        elif d == 1:
+            fields = yr[side, body : body + EX * Y, :].reshape(EX, Y, Z)
+        else:
+            fields = zr[side, packs : packs + EX]
+        return spread_rows(fields, which)
 
     @pl.when(jnp.logical_not(late))
     def _():
-        send_halo(0)
-        send_halo(1)
-
-    send_halo(2)
-
-    @pl.when(ahead & jnp.logical_not(last_x))
+        send_x()
+        send_e()
+        send_y()
+
+    send_z()
+
+    @pl.when(late & jnp.logical_not(last_x))
     def _():
-        for k in (1, -1):
-            if (0, k) in links:
-                await_near(0, k)
-        arrivals["x", 0][0].start()
+        send_x()
 
     @pl.when(late)
     def _():
-        send_halo(1)
+        send_e()
+        send_y()
 
     @pl.when(jnp.logical_not(last_chip))
     def _():
         speed_out()
-
-    @pl.when(ahead)
-    def _():
-        send_halo(0, 1)
-
-    @pl.when(late & jnp.logical_not(ahead))
-    def _():
-        send_halo(0)
-
-    def arrive(*key):
-        for copy in arrivals[key]:
-            copy.wait_recv()
 
     def cyclic_fluxes(d, halo_inputs, number, first):
         n = extent[d]
@@ -521,8 +527,6 @@
         shifts = (-2, -1, 1, 2)
         along = {k: {d: beside(velocity[d], h_vel[d], k)} for k in shifts}
         p_at = {k: beside(pressure, h_p, k) for k in shifts}
-        arrive("e", d, 0)
-        arrive("e", d, 1)
         flag = roll(jnp.where(ix == 0, edge(1, d, 2), walls[d]), -1, d)
         ends = ix & (P_SIZE - 1)
         wall = nodes(jnp.where(ends == P_SIZE - 1, flag, 0.0)) > 0.5
@@ -568,17 +572,16 @@
             else:
                 deltas[slot] += diff - before_diff
 
-    arrive("y", 0)
-    arrive("y", 1)
+    arrive("y")
     for c in range(COMPS):
         hy[c] = own_inputs[c]
         for x in range(X):
-            hy[c, x, Y - 2 : Y, :] = yr[0, c, 2 * x : 2 * x + 2, :]
-            hy[c, x, 0:2, :] = yr[1, c, 2 * x : 2 * x + 2, :]
+            at = 2 * (c * X + x)
+            hy[c, x, Y - 2 : Y, :] = yr[0, at : at + 2, :]
+            hy[c, x, 0:2, :] = yr[1, at : at + 2, :]
     cyclic_fluxes(1, [hy[c] for c in range(COMPS)], 1, True)
 
-    arrive("z", 0)
-    arrive("z", 1)
+    arrive("z")
     merged = [
         jnp.where((lane_index & 3) < 2, zr[0, v][None], zr[1, v][None]) for v in range(packs)
     ]
@@ -591,15 +594,11 @@
         z_halo.append(jnp.concatenate(layers, axis=0))
     cyclic_fluxes(2, z_halo, 0, False)
 
-    for side in (0, 1):
-        arrive("x", side)
-        arrive("e", 0, side)
+    arrive("x")
+    arrive("e")
     sides = []
     for side in (0, 1):
-        inputs = [xsp[side, c] for c in range(SPECIES)]
-        inputs += [xve[side, c] for c in range(3)]
-        inputs.append(xpr[side])
-        halo = conserved_of(inputs)
+        halo = conserved_of([xh[side, c] for c in range(COMPS)])
         _, _, h_inv, h_vel, h_p = primitives(halo)
         sides.append((halo, h_vel, h_p, jnp.abs(h_vel[0]) + sound_of(h_inv, h_p)))
 
@@ -707,19 +706,11 @@
         for value in fields:
             pk[phase, at : at + value.shape[0]] = value
             at += value.shape[0]
-        slot = 16 + 6 * phase
-        for side, k in ((0, 1), (1, -1)):
-            if side == 0 or sizes[0] > 2:
-                arrivals["b", phase, 0, side] = [
-                    send(pk.at[phase], pnx.at[side, phase], slot + side, step(0, k))
-                ]
-            else:
-                arrivals["b", phase, 0, side] = []
+        for side, k in first_sides:
+            remote(pk.at[phase], pnx.at[side, phase], 0, 4, step(0, k)).start()
         for side, k in ((0, 1), (1, -1)):
             rows = pl.ds(Y - P_SIZE, P_SIZE) if side == 0 else pl.ds(0, P_SIZE)
-            arrivals["b", phase, 1, side] = [
-                send(pk.at[phase, :, rows], pny.at[phase, :, rows], slot + 2 + side, step(1, k))
-            ]
+            remote(pk.at[phase, :, rows], pny.at[phase, :, rows], 1, 5, step(1, k)).start()
         items = [value[x : x + 1] for value in fields for x in range(value.shape[0])]
         for v in range(pz.shape[1]):
             packed = jnp.zeros((1, Y, Z), jnp.float32)
@@ -730,9 +721,7 @@
                 packed = jnp.where(inside, moved, packed)
             pz[phase, v] = packed[0]
         for side, k in ((0, 1), (1, -1)):
-            arrivals["b", phase, 2, side] = [
-                send(pz.at[phase], qz.at[side, phase], slot + 4 + side, step(2, k))
-            ]
+            remote(pz.at[phase], qz.at[side, phase], 2, 6, step(2, k)).start()
 
     def unpack(early, late):
         low_density, d_density, rho_bound, p_bound = early
@@ -762,6 +751,8 @@
         )
         spread_start(newton + 1, 0, stats)
         if newton == ITERS - 2:
+            for key in ("x", "y", "z", "e"):
+                sent_all(key)
             share(0, (low_five[0], d_rho, rho_bound, p_bound))
         cross = t_vel[0] * d_five[1] + t_vel[1] * d_five[2] + t_vel[2] * d_five[3]
         speed2 = t_vel[0] * t_vel[0] + t_vel[1] * t_vel[1] + t_vel[2] * t_vel[2]
@@ -772,23 +763,11 @@
         beside = {}
         if newton == ITERS - 1:
             share(1, (t_p, p_scale, mean_square, base))
-            for copy in started:
-                copy.wait_send()
-            for turn in range(ITERS):
-                spread_sent(turn)
-            if relayed:
-
-                @pl.when(origin)
-                def _():
-                    relay_copy.wait_send()
-
-            def arrive_both(d):
-                for phase in (0, 1):
-                    for side in (0, 1):
-                        arrive("b", phase, d, side)
-
-            arrive_both(1)
-            arrive_both(2)
+            for d in range(3):
+                sent_all(("b", d))
+
+            arrive(("b", 1))
+            arrive(("b", 2))
             beside[1] = unpack(
                 *[cut_fields(lambda a, b: pny[phase, a:b]) for phase in (0, 1)]
             )
@@ -805,7 +784,7 @@
                 ]
                 halves.append(cut_fields(lambda a, b: jnp.concatenate(items[a:b], axis=0)))
             beside[2] = unpack(*halves)
-            arrive_both(0)
+            arrive(("b", 0))
             for side in (0, 1):
                 if side == 0 or sizes[0] > 2:
                     beside[0, side] = unpack(
@@ -844,7 +823,7 @@
         )
         bl[e] = jnp.concatenate([few[j * P_SIZE : j * P_SIZE + 1] for j in range(EY)], axis=0)
 
-    spread_sent(ITERS)
+    spread_sent(ITERS, len(groups) - 1)
 
 
 def store(state, weights, state_hbm, weights_hbm, sem):
@@ -868,16 +847,13 @@
         depth = 2 * X + 2 * EX
         edge_packs = -(-depth // (Z // (2 * P_SIZE)))
         vmem = lambda *shape: pltpu.VMEM(shape, jnp.float32)
-        reduce_scratch = []
+        groups = reduce_groups(sizes)
+        dma = pltpu.SemaphoreType.DMA
+        sides = 1 if sizes[0] == 2 else 2
+        rows_scratch = []
         for _ in range(ITERS + 1):
-            for group in reduce_groups(sizes):
-                n = len(group_offsets(sizes, group))
-                reduce_scratch += [
-                    vmem(1, ROW),
-                    vmem(n, ROW),
-                    pltpu.SemaphoreType.DMA(()),
-                    pltpu.SemaphoreType.DMA(()),
-                ]
+            for group in groups:
+                rows_scratch += [vmem(1, ROW), vmem(len(group_offsets(sizes, group)), ROW)]
         state, weights = (
             pl.pallas_call(
                 functools.partial(kernel, sizes),
@@ -888,23 +864,19 @@
                 in_specs=[pl.BlockSpec(memory_space=pltpu.HBM)] * 4,
                 out_specs=[pl.BlockSpec(memory_space=pltpu.VMEM)] * 2,
                 scratch_shapes=[
-                    vmem(SPECIES, X, Y, Z),
-                    vmem(3, X, Y, Z),
-                    vmem(X, Y, Z),
+                    vmem(COMPS, X, Y, Z),
                     pltpu.VMEM((3, EX, EY, EZ), jnp.int32),
-                    pltpu.SemaphoreType.DMA((4,)),
-                    vmem(2, SPECIES, 2, Y, Z),
-                    vmem(2, 3, 2, Y, Z),
-                    vmem(2, 2, Y, Z),
-                    vmem(2, COMPS, 2 * X, Z),
-                    vmem(2, COMPS, 2 * X, Z),
+                    dma((2,)),
+                    vmem(2, COMPS, 2, Y, Z),
+                    vmem(2, COMPS * 2 * X + EX * Y, Z),
+                    vmem(2, COMPS * 2 * X + EX * Y, Z),
                     vmem(COMPS, X, Y, Z),
-                    vmem(packs, Y, Z),
-                    vmem(2, packs, Y, Z),
-                    vmem(3, EX, Y, Z),
-                    vmem(2, 3, EX, Y, Z),
+                    vmem(packs + EX, Y, Z),
+                    vmem(2, packs + EX, Y, Z),
+                    vmem(EX, Y, Z),
+                    vmem(sides, EX, Y, Z),
                     vmem(2, depth, Y, Z),
-                    vmem(2, 2, depth, Y, Z),
+                    vmem(sides, 2, depth, Y, Z),
                     vmem(2, depth, Y, Z),
                     vmem(2, edge_packs, Y, Z),
                     vmem(2, 2, edge_packs, Y, Z),
@@ -913,15 +885,16 @@
                     vmem(2, COMPS, X, Y, Z),
                     vmem(COMPS, X, Y, Z),
                     vmem(COMPS - SPECIES + 1, X, Y, Z),
-                    pltpu.SemaphoreType.DMA((28,)),
-                    pltpu.SemaphoreType.DMA((28,)),
+                    dma((4,)),
+                    dma((7,)),
                     pltpu.SemaphoreType.REGULAR((len(halo_links(sizes)),)),
                     pltpu.SemaphoreType.REGULAR,
                     vmem(1, ROW),
-                    pltpu.SemaphoreType.DMA(()),
-                    pltpu.SemaphoreType.DMA(()),
+                    dma(()),
+                    dma(()),
+                    dma((2 * len(groups),)),
                 ]
-                + reduce_scratch,
+                + rows_scratch,
                 compiler_params=pltpu.CompilerParams(collective_id=0, has_side_effects=True),
             )(species, velocity_in, pressure_in, wall_types)
         )

time: 21.7 us -> 21.3 us (0.982)
  Pallas kernels: 20.9 us -> 20.5 us
    pallas_call x1, Pallas kernels: 20.3 us -> 19.8 us  [local(): pl.pallas_call(functools.partial(kernel, sizes), out_shape=[pltpu.VMEM((C...]
where the time goes in v4:
time: 21.3 us; the launch traced here: 21.1 us
  Pallas kernels  20.5 us (96%)
  between operations  0.64 us (3%)
    pallas_call x1, Pallas kernels, local(): pl.pallas_call(functools.partial(kernel, sizes), out_shape=[pltpu.VMEM((C...  19.8 us
    pallas_call x1, Pallas kernels, local(): pl.pallas_call(store, out_shape=[jax.ShapeDtypeStruct((COMPS, X, Y, Z), j...  0.68 us

profile of v4, /device:TPU:0, one launch (start us, length us, event | category | flops | bytes accessed | tf_op | source)
XLA Modules:
  0.0 21.1 jit_solution(2077060678109712023)
XLA Ops:
  0.6 19.8 %shard_map.59 = (f32[9,4,8,128]{3,2,1,0:T(8,128)S(1)}, f32[1,2,32]{2,1,0:T(2,128)S(1)}) custom-call(f32[5,4,8,128]{3,2,1,0:T(8,128)} %sp_hbm.1, f32[3,4,8,128]{3,2,1,0:T(8,128)} %ve_hbm.1, f32[4,8,128]{2,1,0:T(8,128)} %pr_hbm.1, s32[3,1,2,32]{3,2,1,0:T(2,128)} %wa_hbm.1), custom_call_target="tpu_custom_call" | custom-call | tf_op jit(solution)/shard_map/pallas_call | solution.py:858
  20.5 0.7 %shard_map.60 = (f32[9,4,8,128]{3,2,1,0:T(8,128)}, f32[1,2,32]{2,1,0:T(2,128)}) custom-call(f32[9,4,8,128]{3,2,1,0:T(8,128)S(1)} %get-tuple-element.4.state, f32[1,2,32]{2,1,0:T(2,128)S(1)} %get-tuple-element.5.weights), custom_call_target="tpu_custom_call" | custom-call | tf_op jit(solution)/shard_map/pallas_call | solution.py:902

commit v5 on v4

--- a/solution.py
+++ b/solution.py
@@ -97,7 +97,7 @@
 
 def kernel(
     sizes, sp_hbm, ve_hbm, pr_hbm, wa_hbm, out, bl, inp, wa, load_sem,
-    xh, ys, yr, hy, zs, zr, es, er, pk, pnx, pny, pz, qz, dx, du, dw, lows, deltas,
+    xh, ys, yr, hy, zs, zr, es, er, pk, pnx, pny, pz, qz, bs, bc, dx, du, dw, lows, deltas,
     sent_sem, came_sem, near_sem, all_sem, relay, relay_sem, row_sent, row_came, *rows_scratch
 ):
     X, Y, Z = inp.shape[1:]
@@ -195,6 +195,7 @@
             pl.semaphore_wait(all_sem, 1)
 
     pltpu.make_async_copy(inp, inp, load_sem.at[0]).wait()
+    loads[3].wait()
 
     origin = (me[0] == 0) & (me[1] <= 1)
     next_up = origin & (me[2] == 1)
@@ -373,8 +374,9 @@
         "z": (zr, 2, 2),
         "e": (er, 3, 3),
         ("b", 0): (pnx, 0, 4),
-        ("b", 1): (pny.at[:, :, pl.ds(0, 2 * P_SIZE)], 1, 5),
+        ("b", 1): (pny, 1, 5),
         ("b", 2): (qz, 2, 6),
+        "c": (bc, 3, 7),
     }
 
     def whole(key):
@@ -459,7 +461,6 @@
         lax.broadcasted_iota(jnp.int32, (Y, EY), 0) // P_SIZE
         == lax.broadcasted_iota(jnp.int32, (Y, EY), 1)
     ).astype(jnp.float32)
-    loads[3].wait()
     walls = []
     for d in range(3):
         layers = []
@@ -667,8 +668,6 @@
 
     low_five = [u - ratio * f for u, f in zip(five(cons), fluxes)]
     d_five = [-(ratio * d) for d in jumps]
-    low_safe, _, low_pressure = state_of(low_five[0], low_five[1:4], low_five[4])
-    low_sigma = entropy(low_five[0], low_safe, low_pressure)
     d_rho = d_five[0]
     rho_scale = 1.0 / jnp.maximum(-d_rho, SLOPE_FLOOR)
     count = X * Y * Z * sizes[0] * sizes[1] * sizes[2]
@@ -699,51 +698,79 @@
         return jnp.maximum(jnp.minimum(cap, base + lowered), 0.0)
 
     per_edge = Z // (2 * P_SIZE)
-    depth = 2 * X + 2 * EX
-
-    def share(phase, fields):
+    depth = 10 * X + 2 * EX
+
+    def share(fields):
         at = 0
         for value in fields:
-            pk[phase, at : at + value.shape[0]] = value
+            pk[at : at + value.shape[0]] = value
             at += value.shape[0]
         for side, k in first_sides:
-            remote(pk.at[phase], pnx.at[side, phase], 0, 4, step(0, k)).start()
+            remote(pk, pnx.at[side], 0, 4, step(0, k)).start()
         for side, k in ((0, 1), (1, -1)):
             rows = pl.ds(Y - P_SIZE, P_SIZE) if side == 0 else pl.ds(0, P_SIZE)
-            remote(pk.at[phase, :, rows], pny.at[phase, :, rows], 1, 5, step(1, k)).start()
+            remote(pk.at[:, rows], pny.at[:, rows], 1, 5, step(1, k)).start()
         items = [value[x : x + 1] for value in fields for x in range(value.shape[0])]
-        for v in range(pz.shape[1]):
+        for v in range(pz.shape[0]):
             packed = jnp.zeros((1, Y, Z), jnp.float32)
             for j, item in enumerate(items[v * per_edge : (v + 1) * per_edge]):
                 at = 2 * P_SIZE * j
                 moved = roll(item, at + P_SIZE, 2)
                 inside = (lane_index >= at) & (lane_index < at + 2 * P_SIZE)
                 packed = jnp.where(inside, moved, packed)
-            pz[phase, v] = packed[0]
+            pz[v] = packed[0]
         for side, k in ((0, 1), (1, -1)):
-            remote(pz.at[phase], qz.at[side, phase], 2, 6, step(2, k)).start()
-
-    def unpack(early, late):
-        low_density, d_density, rho_bound, p_bound = early
-        t_p, p_scale, mean_square, base = late
-        t_density = low_density + nodes(base) * d_density
-        scale = 1.0 / jnp.maximum(-d_density, SLOPE_FLOOR)
-        return t_density, scale, t_p, p_scale, rho_bound, p_bound, mean_square, base
-
-    def cut_fields(layer):
-        ends = (0, X, 2 * X, 2 * X + EX, depth)
-        return [layer(a, b) for a, b in zip(ends[:-1], ends[1:])]
-
+            remote(pz, qz.at[side], 2, 6, step(2, k)).start()
+
+    sides_x = len(first_sides)
+
+    def share_blend():
+        bs[...] = blend
+        for side, k in first_sides:
+            there = bc.at[pl.ds(side * EX, EX)]
+            remote(bs, there, 3, 7, step(0, k)).start()
+        for side, k in ((0, 1), (1, -1)):
+            there = bc.at[pl.ds((sides_x + 1 + side) * EX, EX)]
+            remote(bs, there, 3, 7, step(2, k)).start()
+            rows = pl.ds(Y - P_SIZE, P_SIZE) if side == 0 else pl.ds(0, P_SIZE)
+            there = bc.at[pl.ds(sides_x * EX, EX), rows]
+            remote(bs.at[:, rows], there, 3, 7, step(1, k)).start()
+
+    def trial_of(low, d, low_sigma, blend):
+        weight = None if blend is None else nodes(blend)
+        trial = [a + (b if weight is None else weight * b) for a, b in zip(low, d)]
+        safe, speeds, p = state_of(trial[0], trial[1:4], trial[4])
+        residual = entropy(trial[0], safe, p) - low_sigma
+        return trial[0], speeds, p, residual * residual
+
+    def scales_of(d, speeds, square):
+        cross = speeds[0] * d[1] + speeds[1] * d[2] + speeds[2] * d[3]
+        speed2 = speeds[0] * speeds[0] + speeds[1] * speeds[1] + speeds[2] * speeds[2]
+        slope = (GAMMA - 1.0) * (d[4] - cross + 0.5 * speed2 * d[0])
+        mean_square = element(square, jnp.add) * (1.0 / (P_SIZE**3))
+        return 1.0 / jnp.maximum(-slope, SLOPE_FLOOR), mean_square
+
+    def sigma_of(low):
+        safe, _, p = state_of(low[0], low[1:4], low[4])
+        return entropy(low[0], safe, p)
+
+    def neighbour_low(layer):
+        low = [layer(i * X, (i + 1) * X) for i in range(5)]
+        d = [layer(i * X, (i + 1) * X) for i in range(5, 10)]
+        bounds = [layer(10 * X + i * EX, 10 * X + (i + 1) * EX) for i in range(2)]
+        scale = 1.0 / jnp.maximum(-d[0], SLOPE_FLOOR)
+        return low, d, sigma_of(low), scale, bounds
+
+    def neighbour_fields(known, blend):
+        low, d, sigma, scale, bounds = known
+        density, speeds, p, square = trial_of(low, d, sigma, blend)
+        p_scale, mean_square = scales_of(d, speeds, square)
+        return density, scale, p, p_scale, bounds[0], bounds[1], mean_square, blend
+
+    low_sigma = sigma_of(low_five)
     blend = None
     for newton in range(ITERS):
-        blend_nodes = None if blend is None else nodes(blend)
-        trial = [
-            low + (d if blend is None else blend_nodes * d) for low, d in zip(low_five, d_five)
-        ]
-        t_density = trial[0]
-        t_safe, t_vel, t_p = state_of(t_density, trial[1:4], trial[4])
-        residual = entropy(t_density, t_safe, t_p) - low_sigma
-        square = residual * residual
+        t_density, t_vel, t_p, square = trial_of(low_five, d_five, low_sigma, blend)
         stats = jnp.where(
             stat_lane == 0,
             total(t_density, jnp.minimum),
@@ -753,47 +780,42 @@
         if newton == ITERS - 2:
             for key in ("x", "y", "z", "e"):
                 sent_all(key)
-            share(0, (low_five[0], d_rho, rho_bound, p_bound))
-        cross = t_vel[0] * d_five[1] + t_vel[1] * d_five[2] + t_vel[2] * d_five[3]
-        speed2 = t_vel[0] * t_vel[0] + t_vel[1] * t_vel[1] + t_vel[2] * t_vel[2]
-        slope = (GAMMA - 1.0) * (d_five[4] - cross + 0.5 * speed2 * d_rho)
-        p_scale = 1.0 / jnp.maximum(-slope, SLOPE_FLOOR)
-        mean_square = element(square, jnp.add) * (1.0 / (P_SIZE**3))
+            share((*low_five, *d_five, rho_bound, p_bound))
+        p_scale, mean_square = scales_of(d_five, t_vel, square)
         base = jnp.ones((EX, Y, Z), jnp.float32) if blend is None else blend
         beside = {}
         if newton == ITERS - 1:
-            share(1, (t_p, p_scale, mean_square, base))
+            for d in (1, 2, 0):
+                arrive(("b", d))
+            known = {1: neighbour_low(lambda a, b: pny[a:b])}
+            near = (lane_index & (2 * P_SIZE - 1)) < P_SIZE
+            edges = [
+                jnp.where(near, qz[0, v][None], qz[1, v][None]) for v in range(pz.shape[0])
+            ]
+            items = [
+                roll(edges[j // per_edge], -(2 * P_SIZE * (j % per_edge) + P_SIZE), 2)
+                for j in range(depth)
+            ]
+            known[2] = neighbour_low(lambda a, b: jnp.concatenate(items[a:b], axis=0))
+            for side in range(sides_x):
+                known[0, side] = neighbour_low(lambda a, b: pnx[side, a:b])
             for d in range(3):
                 sent_all(("b", d))
-
-            arrive(("b", 1))
-            arrive(("b", 2))
-            beside[1] = unpack(
-                *[cut_fields(lambda a, b: pny[phase, a:b]) for phase in (0, 1)]
+            sent_all("c")
+            arrive("c")
+            at = sides_x * EX
+            weights = {(0, side): bc[side * EX : (side + 1) * EX] for side in range(sides_x)}
+            weights[1] = bc[at : at + EX]
+            weights[2] = jnp.where(
+                lane_index < P_SIZE, bc[at + 2 * EX : at + 3 * EX], bc[at + EX : at + 2 * EX]
             )
-            near = (lane_index & (2 * P_SIZE - 1)) < P_SIZE
-            halves = []
-            for phase in (0, 1):
-                edges = [
-                    jnp.where(near, qz[0, phase, v][None], qz[1, phase, v][None])
-                    for v in range(pz.shape[1])
-                ]
-                items = [
-                    roll(edges[j // per_edge], -(2 * P_SIZE * (j % per_edge) + P_SIZE), 2)
-                    for j in range(depth)
-                ]
-                halves.append(cut_fields(lambda a, b: jnp.concatenate(items[a:b], axis=0)))
-            beside[2] = unpack(*halves)
-            arrive(("b", 0))
-            for side in (0, 1):
-                if side == 0 or sizes[0] > 2:
-                    beside[0, side] = unpack(
-                        *[cut_fields(lambda a, b: pnx[side, phase, a:b]) for phase in (0, 1)]
-                    )
+            beside = {key: neighbour_fields(known[key], weights[key]) for key in known}
         got = broadcast_stats(spread_end(newton + 1, combine_stats))
         blend = next_blend(
             got, (t_density, rho_scale, t_p, p_scale, rho_bound, p_bound, mean_square, base)
         )
+        if newton == ITERS - 2:
+            share_blend()
 
     beside = {key: next_blend(got, packed) for key, packed in beside.items()}
     beside.setdefault((0, 1), beside[0, 0])
@@ -844,7 +866,7 @@
         X, Y, Z = pressure_in.shape
         EX, EY, EZ = wall_types.shape[1:]
         packs = -(-COMPS // (Z // (4 * X)))
-        depth = 2 * X + 2 * EX
+        depth = 10 * X + 2 * EX
         edge_packs = -(-depth // (Z // (2 * P_SIZE)))
         vmem = lambda *shape: pltpu.VMEM(shape, jnp.float32)
         groups = reduce_groups(sizes)
@@ -875,18 +897,20 @@
                     vmem(2, packs + EX, Y, Z),
                     vmem(EX, Y, Z),
                     vmem(sides, EX, Y, Z),
-                    vmem(2, depth, Y, Z),
-                    vmem(sides, 2, depth, Y, Z),
-                    vmem(2, depth, Y, Z),
+                    vmem(depth, Y, Z),
+                    vmem(sides, depth, Y, Z),
+                    vmem(depth, Y, Z),
+                    vmem(edge_packs, Y, Z),
                     vmem(2, edge_packs, Y, Z),
-                    vmem(2, 2, edge_packs, Y, Z),
+                    vmem(EX, Y, Z),
+                    vmem((sides + 3) * EX, Y, Z),
                     vmem(COMPS, X + 1, Y, Z),
                     vmem(2, COMPS, X, Y, Z),
                     vmem(2, COMPS, X, Y, Z),
                     vmem(COMPS, X, Y, Z),
                     vmem(COMPS - SPECIES + 1, X, Y, Z),
                     dma((4,)),
-                    dma((7,)),
+                    dma((8,)),
                     pltpu.SemaphoreType.REGULAR((len(halo_links(sizes)),)),
                     pltpu.SemaphoreType.REGULAR,
                     vmem(1, ROW),

time: 21.3 us -> 21.2 us (level)
  no operation moved by 1% of the time
where the time goes in v5:
time: 21.2 us; the launch traced here: 21 us
  Pallas kernels  20.4 us (96%)
  between operations  0.64 us (3%)
    pallas_call x1, Pallas kernels, local(): pl.pallas_call(functools.partial(kernel, sizes), out_shape=[pltpu.VMEM((C...  19.7 us
    pallas_call x1, Pallas kernels, local(): pl.pallas_call(store, out_shape=[jax.ShapeDtypeStruct((COMPS, X, Y, Z), j...  0.68 us

profile of v5, /device:TPU:0, one launch (start us, length us, event | category | flops | bytes accessed | tf_op | source)
XLA Modules:
  0.0 21.0 jit_solution(15631109638004699448)
XLA Ops:
  0.6 19.7 %shard_map.59 = (f32[9,4,8,128]{3,2,1,0:T(8,128)S(1)}, f32[1,2,32]{2,1,0:T(2,128)S(1)}) custom-call(f32[5,4,8,128]{3,2,1,0:T(8,128)} %sp_hbm.1, f32[3,4,8,128]{3,2,1,0:T(8,128)} %ve_hbm.1, f32[4,8,128]{2,1,0:T(8,128)} %pr_hbm.1, s32[3,1,2,32]{3,2,1,0:T(2,128)} %wa_hbm.1), custom_call_target="tpu_custom_call" | custom-call | tf_op jit(solution)/shard_map/pallas_call | solution.py:880
  20.3 0.7 %shard_map.60 = (f32[9,4,8,128]{3,2,1,0:T(8,128)}, f32[1,2,32]{2,1,0:T(2,128)}) custom-call(f32[9,4,8,128]{3,2,1,0:T(8,128)S(1)} %get-tuple-element.4.state, f32[1,2,32]{2,1,0:T(2,128)S(1)} %get-tuple-element.5.weights), custom_call_target="tpu_custom_call" | custom-call | tf_op jit(solution)/shard_map/pallas_call | solution.py:926

commit v6 on v5

--- a/solution.py
+++ b/solution.py
@@ -419,7 +419,7 @@
                     rows_scratch[0][...] = speed_row
                     relay_copy.start()
 
-    @pl.when(late & last_x & jnp.logical_not(last_chip))
+    @pl.when(last_x & jnp.logical_not(last_chip))
     def _():
         send_x()
 
@@ -492,9 +492,12 @@
             fields = zr[side, packs : packs + EX]
         return spread_rows(fields, which)
 
+    @pl.when(jnp.logical_not(late | last_x))
+    def _():
+        send_x()
+
     @pl.when(jnp.logical_not(late))
     def _():
-        send_x()
         send_e()
         send_y()
 
@@ -835,14 +838,9 @@
             change += upper * du[number, c] - lower * dw[number, c]
         out[c] = cons[c] - ratio * change
 
-    pick_lanes = (
-        lax.broadcasted_iota(jnp.int32, (Z, EZ), 1) * P_SIZE
-        == lax.broadcasted_iota(jnp.int32, (Z, EZ), 0)
-    ).astype(jnp.float32)
+    chosen = (lax.broadcasted_iota(jnp.int32, (Y, Z), 1) * P_SIZE) & (Z - 1)
     for e in range(EX):
-        few = jnp.dot(
-            blend[e], pick_lanes, preferred_element_type=jnp.float32, precision=lax.Precision.HIGHEST
-        )
+        few = jnp.take_along_axis(blend[e], chosen, axis=1, mode="promise_in_bounds")[:, :EZ]
         bl[e] = jnp.concatenate([few[j * P_SIZE : j * P_SIZE + 1] for j in range(EY)], axis=0)
 
     spread_sent(ITERS, len(groups) - 1)

time: 21.2 us -> 21.1 us (level)
  no operation moved by 1% of the time
where the time goes in v6:
time: 21.1 us; the launch traced here: 21 us
  Pallas kernels  20.3 us (96%)
  between operations  0.64 us (3%)
    pallas_call x1, Pallas kernels, local(): pl.pallas_call(functools.partial(kernel, sizes), out_shape=[pltpu.VMEM((C...  19.7 us
    pallas_call x1, Pallas kernels, local(): pl.pallas_call(store, out_shape=[jax.ShapeDtypeStruct((COMPS, X, Y, Z), j...  0.68 us

profile of v6, /device:TPU:0, one launch (start us, length us, event | category | flops | bytes accessed | tf_op | source)
XLA Modules:
  0.0 21.0 jit_solution(14281993817981365878)
XLA Ops:
  0.6 19.7 %shard_map.59 = (f32[9,4,8,128]{3,2,1,0:T(8,128)S(1)}, f32[1,2,32]{2,1,0:T(2,128)S(1)}) custom-call(f32[5,4,8,128]{3,2,1,0:T(8,128)} %sp_hbm.1, f32[3,4,8,128]{3,2,1,0:T(8,128)} %ve_hbm.1, f32[4,8,128]{2,1,0:T(8,128)} %pr_hbm.1, s32[3,1,2,32]{3,2,1,0:T(2,128)} %wa_hbm.1), custom_call_target="tpu_custom_call" | custom-call | tf_op jit(solution)/shard_map/pallas_call | solution.py:878
  20.3 0.7 %shard_map.60 = (f32[9,4,8,128]{3,2,1,0:T(8,128)}, f32[1,2,32]{2,1,0:T(2,128)}) custom-call(f32[9,4,8,128]{3,2,1,0:T(8,128)S(1)} %get-tuple-element.4.state, f32[1,2,32]{2,1,0:T(2,128)S(1)} %get-tuple-element.5.weights), custom_call_target="tpu_custom_call" | custom-call | tf_op jit(solution)/shard_map/pallas_call | solution.py:924

commit v7 on v6

--- a/solution.py
+++ b/solution.py
@@ -97,7 +97,7 @@
 
 def kernel(
     sizes, sp_hbm, ve_hbm, pr_hbm, wa_hbm, out, bl, inp, wa, load_sem,
-    xh, ys, yr, hy, zs, zr, es, er, pk, pnx, pny, pz, qz, bs, bc, dx, du, dw, lows, deltas,
+    xh, ys, yr, hy, zs, zr, es, er, pk, nb, pz, bs, bc, dx, du, dw, lows, deltas,
     sent_sem, came_sem, near_sem, all_sem, relay, relay_sem, row_sent, row_came, *rows_scratch
 ):
     X, Y, Z = inp.shape[1:]
@@ -373,10 +373,8 @@
         "y": (yr, 1, 1),
         "z": (zr, 2, 2),
         "e": (er, 3, 3),
-        ("b", 0): (pnx, 0, 4),
-        ("b", 1): (pny, 1, 5),
-        ("b", 2): (qz, 2, 6),
-        "c": (bc, 3, 7),
+        "b": (nb, 0, 4),
+        "c": (bc, 3, 5),
     }
 
     def whole(key):
@@ -702,6 +700,7 @@
 
     per_edge = Z // (2 * P_SIZE)
     depth = 10 * X + 2 * EX
+    sides_x = len(first_sides)
 
     def share(fields):
         at = 0
@@ -709,10 +708,11 @@
             pk[at : at + value.shape[0]] = value
             at += value.shape[0]
         for side, k in first_sides:
-            remote(pk, pnx.at[side], 0, 4, step(0, k)).start()
+            remote(pk, nb.at[pl.ds(side * depth, depth)], 0, 4, step(0, k)).start()
         for side, k in ((0, 1), (1, -1)):
             rows = pl.ds(Y - P_SIZE, P_SIZE) if side == 0 else pl.ds(0, P_SIZE)
-            remote(pk.at[:, rows], pny.at[:, rows], 1, 5, step(1, k)).start()
+            there = nb.at[pl.ds(sides_x * depth, depth), rows]
+            remote(pk.at[:, rows], there, 0, 4, step(1, k)).start()
         items = [value[x : x + 1] for value in fields for x in range(value.shape[0])]
         for v in range(pz.shape[0]):
             packed = jnp.zeros((1, Y, Z), jnp.float32)
@@ -723,21 +723,20 @@
                 packed = jnp.where(inside, moved, packed)
             pz[v] = packed[0]
         for side, k in ((0, 1), (1, -1)):
-            remote(pz, qz.at[side], 2, 6, step(2, k)).start()
-
-    sides_x = len(first_sides)
+            there = nb.at[pl.ds((sides_x + 1) * depth + side * pz.shape[0], pz.shape[0])]
+            remote(pz, there, 0, 4, step(2, k)).start()
 
     def share_blend():
         bs[...] = blend
         for side, k in first_sides:
             there = bc.at[pl.ds(side * EX, EX)]
-            remote(bs, there, 3, 7, step(0, k)).start()
+            remote(bs, there, 3, 5, step(0, k)).start()
         for side, k in ((0, 1), (1, -1)):
             there = bc.at[pl.ds((sides_x + 1 + side) * EX, EX)]
-            remote(bs, there, 3, 7, step(2, k)).start()
+            remote(bs, there, 3, 5, step(2, k)).start()
             rows = pl.ds(Y - P_SIZE, P_SIZE) if side == 0 else pl.ds(0, P_SIZE)
             there = bc.at[pl.ds(sides_x * EX, EX), rows]
-            remote(bs.at[:, rows], there, 3, 7, step(1, k)).start()
+            remote(bs.at[:, rows], there, 3, 5, step(1, k)).start()
 
     def trial_of(low, d, low_sigma, blend):
         weight = None if blend is None else nodes(blend)
@@ -788,12 +787,15 @@
         base = jnp.ones((EX, Y, Z), jnp.float32) if blend is None else blend
         beside = {}
         if newton == ITERS - 1:
-            for d in (1, 2, 0):
-                arrive(("b", d))
-            known = {1: neighbour_low(lambda a, b: pny[a:b])}
+            arrive("b")
+            at = sides_x * depth
+            known = {1: neighbour_low(lambda a, b: nb[at + a : at + b])}
+            ends = [
+                nb[at + depth + i * pz.shape[0] : at + depth + (i + 1) * pz.shape[0]] for i in (0, 1)
+            ]
             near = (lane_index & (2 * P_SIZE - 1)) < P_SIZE
             edges = [
-                jnp.where(near, qz[0, v][None], qz[1, v][None]) for v in range(pz.shape[0])
+                jnp.where(near, ends[0][v][None], ends[1][v][None]) for v in range(pz.shape[0])
             ]
             items = [
                 roll(edges[j // per_edge], -(2 * P_SIZE * (j % per_edge) + P_SIZE), 2)
@@ -801,9 +803,9 @@
             ]
             known[2] = neighbour_low(lambda a, b: jnp.concatenate(items[a:b], axis=0))
             for side in range(sides_x):
-                known[0, side] = neighbour_low(lambda a, b: pnx[side, a:b])
-            for d in range(3):
-                sent_all(("b", d))
+                start = side * depth
+                known[0, side] = neighbour_low(lambda a, b: nb[start + a : start + b])
+            sent_all("b")
             sent_all("c")
             arrive("c")
             at = sides_x * EX
@@ -847,14 +849,12 @@
 
 
 def store(state, weights, state_hbm, weights_hbm, sem):
-    copies = [
-        pltpu.make_async_copy(state, state_hbm, sem.at[0]),
-        pltpu.make_async_copy(weights, weights_hbm, sem.at[1]),
-    ]
-    for copy in copies:
-        copy.start()
-    for copy in copies:
-        copy.wait()
+    small = pltpu.make_async_copy(weights, weights_hbm, sem.at[1])
+    small.start()
+    for c in range(0, COMPS, 3):
+        pltpu.make_async_copy(state.at[c : c + 3], state_hbm.at[c : c + 3], sem.at[0]).start()
+    pltpu.make_async_copy(state, state_hbm, sem.at[0]).wait()
+    small.wait()
 
 
 def solution(mesh):
@@ -896,10 +896,8 @@
                     vmem(EX, Y, Z),
                     vmem(sides, EX, Y, Z),
                     vmem(depth, Y, Z),
-                    vmem(sides, depth, Y, Z),
-                    vmem(depth, Y, Z),
+                    vmem((sides + 1) * depth + 2 * edge_packs, Y, Z),
                     vmem(edge_packs, Y, Z),
-                    vmem(2, edge_packs, Y, Z),
                     vmem(EX, Y, Z),
                     vmem((sides + 3) * EX, Y, Z),
                     vmem(COMPS, X + 1, Y, Z),
@@ -908,7 +906,7 @@
                     vmem(COMPS, X, Y, Z),
                     vmem(COMPS - SPECIES + 1, X, Y, Z),
                     dma((4,)),
-                    dma((8,)),
+                    dma((6,)),
                     pltpu.SemaphoreType.REGULAR((len(halo_links(sizes)),)),
                     pltpu.SemaphoreType.REGULAR,
                     vmem(1, ROW),

time: 21.1 us -> 21.1 us (level)
  no operation moved by 1% of the time
where the time goes in v7:
time: 21.1 us; the launch traced here: 21 us
  Pallas kernels  20.3 us (96%)
  between operations  0.64 us (3%)
    pallas_call x1, Pallas kernels, local(): pl.pallas_call(functools.partial(kernel, sizes), out_shape=[pltpu.VMEM((C...  19.6 us
    pallas_call x1, Pallas kernels, local(): pl.pallas_call(store, out_shape=[jax.ShapeDtypeStruct((COMPS, X, Y, Z), j...  0.68 us

profile of v7, /device:TPU:0, one launch (start us, length us, event | category | flops | bytes accessed | tf_op | source)
XLA Modules:
  0.0 21.0 jit_solution(4983010850237700212)
XLA Ops:
  0.6 19.6 %shard_map.59 = (f32[9,4,8,128]{3,2,1,0:T(8,128)S(1)}, f32[1,2,32]{2,1,0:T(2,128)S(1)}) custom-call(f32[5,4,8,128]{3,2,1,0:T(8,128)} %sp_hbm.1, f32[3,4,8,128]{3,2,1,0:T(8,128)} %ve_hbm.1, f32[4,8,128]{2,1,0:T(8,128)} %pr_hbm.1, s32[3,1,2,32]{3,2,1,0:T(2,128)} %wa_hbm.1), custom_call_target="tpu_custom_call" | custom-call | tf_op jit(solution)/shard_map/pallas_call | solution.py:878
  20.3 0.7 %shard_map.60 = (f32[9,4,8,128]{3,2,1,0:T(8,128)}, f32[1,2,32]{2,1,0:T(2,128)}) custom-call(f32[9,4,8,128]{3,2,1,0:T(8,128)S(1)} %get-tuple-element.4.state, f32[1,2,32]{2,1,0:T(2,128)S(1)} %get-tuple-element.5.weights), custom_call_target="tpu_custom_call" | custom-call | tf_op jit(solution)/shard_map/pallas_call | solution.py:922

commit v8 on v7

--- a/solution.py
+++ b/solution.py
@@ -98,7 +98,7 @@
 def kernel(
     sizes, sp_hbm, ve_hbm, pr_hbm, wa_hbm, out, bl, inp, wa, load_sem,
     xh, ys, yr, hy, zs, zr, es, er, pk, nb, pz, bs, bc, dx, du, dw, lows, deltas,
-    sent_sem, came_sem, near_sem, all_sem, relay, relay_sem, row_sent, row_came, *rows_scratch
+    sent_sem, came_sem, near_sem, all_sem, row_sent, row_came, *rows_scratch
 ):
     X, Y, Z = inp.shape[1:]
     EX, EY, EZ = wa.shape[1:]
@@ -121,7 +121,8 @@
     def step(d, k):
         return tuple(k % sizes[d] if a == d else 0 for a in range(3))
 
-    relayed = len(groups) == 1
+    relayed = False
+    relay = relay_sem = None
     if relayed:
         rows_scratch[1][...] = jnp.zeros_like(rows_scratch[1])
 
@@ -909,8 +910,6 @@
                     dma((6,)),
                     pltpu.SemaphoreType.REGULAR((len(halo_links(sizes)),)),
                     pltpu.SemaphoreType.REGULAR,
-                    vmem(1, ROW),
-                    dma(()),
                     dma(()),
                     dma((2 * len(groups),)),
                 ]

time: 21.1 us -> 21.1 us (level)
  no operation moved by 1% of the time
where the time goes in v8:
time: 21.1 us; the launch traced here: 21 us
  Pallas kernels  20.3 us (96%)
  between operations  0.64 us (3%)
    pallas_call x1, Pallas kernels, local(): pl.pallas_call(functools.partial(kernel, sizes), out_shape=[pltpu.VMEM((C...  19.6 us
    pallas_call x1, Pallas kernels, local(): pl.pallas_call(store, out_shape=[jax.ShapeDtypeStruct((COMPS, X, Y, Z), j...  0.68 us

profile of v8, /device:TPU:0, one launch (start us, length us, event | category | flops | bytes accessed | tf_op | source)
XLA Modules:
  0.0 21.0 jit_solution(6333650857119449087)
XLA Ops:
  0.6 19.6 %shard_map.59 = (f32[9,4,8,128]{3,2,1,0:T(8,128)S(1)}, f32[1,2,32]{2,1,0:T(2,128)S(1)}) custom-call(f32[5,4,8,128]{3,2,1,0:T(8,128)} %sp_hbm.1, f32[3,4,8,128]{3,2,1,0:T(8,128)} %ve_hbm.1, f32[4,8,128]{2,1,0:T(8,128)} %pr_hbm.1, s32[3,1,2,32]{3,2,1,0:T(2,128)} %wa_hbm.1), custom_call_target="tpu_custom_call" | custom-call | tf_op jit(solution)/shard_map/pallas_call | solution.py:879
  20.3 0.7 %shard_map.60 = (f32[9,4,8,128]{3,2,1,0:T(8,128)}, f32[1,2,32]{2,1,0:T(2,128)}) custom-call(f32[9,4,8,128]{3,2,1,0:T(8,128)S(1)} %get-tuple-element.4.state, f32[1,2,32]{2,1,0:T(2,128)S(1)} %get-tuple-element.5.weights), custom_call_target="tpu_custom_call" | custom-call | tf_op jit(solution)/shard_map/pallas_call | solution.py:921
